TPU v7x, 32 devices: a whole 2x2x4 slice. The times are simulated.
32 devices in a mesh: cfg: 2 (over x), seq: 8 (over z, y), dp: 2 (over core).
Axes of the slice: x: 2, y: 2, z: 4, core: 2. Of those that a mesh axis runs over, the one named last changes fastest.
Arguments:
- teacher_query: bfloat16 [2, 2, 2, 1024, 2048], P('cfg', None, 'dp', 'seq'), may hold values from -6 to 6
- teacher_key: bfloat16 [2, 2, 2, 1024, 2048], P('cfg', None, 'dp', 'seq'), may hold values from -6 to 6
- teacher_value: bfloat16 [2, 2, 2, 1024, 2048], P('cfg', None, 'dp', 'seq'), may hold values from -6 to 6
- hidden: bfloat16 [2, 2, 1024, 3072], P('cfg', 'dp', 'seq'), may hold values from -6 to 6
- adapter_down_weight: bfloat16 [3, 3072, 128], replicated, may hold values from -0.109375 to 0.109375
- adapter_up_weight: bfloat16 [3, 128, 2048], replicated, may hold values from -0.5 to 0.5
- guidance_index: int32 [2, 2], P(None, 'dp'), may hold values from 0 to 7
- timestep_index: int32 [2, 2], P(None, 'dp'), may hold values from 0 to 999
Outputs:
- student_out: bfloat16 [2, 2, 1024, 2048], P('cfg', 'dp', 'seq')
- grad_down: float32 [3, 3072, 128], P(None, ('cfg', 'seq', 'dp'))
- grad_up: float32 [3, 128, 2048], P(None, ('cfg', 'dp'), 'seq')
All inputs are finite; a program needn't handle non-finite values.
Results may differ from a plain program's by a relative error of at most 0.02.
The roundings to bfloat16 on the way count: a program that leaves them out, or rounds other values in their place, can miss the bound.
Values may be sent and summed in bfloat16 or wider, within the bound.
A program may use at most 128 MiB of HBM per device.

v0:
```python
import math

import jax
import jax.numpy as jnp
from jax import lax
from jax.sharding import PartitionSpec as P

HDIM = 128
ADAPTER_RANK = 128
TSTEPS = 1000


def passed_along(value, axis, steps):
    count = lax.axis_size(axis)
    leading, last = (max(0, -steps), min(count, count - steps))
    return lax.ppermute(value, axis, [(source, source + steps) for source in range(leading, last)])


def head_probs(query_block, key_heads, factor):
    scores = (
        jnp.einsum("qhd,khd->hqk", query_block, key_heads, preferred_element_type=jnp.float32)
        * factor
    )
    highest = jnp.max(scores, axis=-1, keepdims=True)
    raised = jnp.exp(scores - highest)
    return raised / jnp.sum(raised, axis=-1, keepdims=True)


def attention_forward(queries, keys, values):
    length, columns_all = queries.shape
    heads_here = columns_all // HDIM
    factor = HDIM ** (-0.5)
    step_rows = min(512, length)
    key_heads = keys.reshape(length, heads_here, HDIM)
    value_heads = values.reshape(length, heads_here, HDIM)
    query_blocks = queries.reshape(length // step_rows, step_rows, heads_here, HDIM)

    def one_block(query_block):
        weights = head_probs(query_block, key_heads, factor).astype(jnp.bfloat16)
        return jnp.einsum("hqk,khd->qhd", weights, value_heads, preferred_element_type=jnp.float32)

    return lax.map(one_block, query_blocks).reshape(length, columns_all)


def attention_backward(queries, keys, values, upstream):
    length, columns_all = queries.shape
    heads_here = columns_all // HDIM
    factor = HDIM ** (-0.5)
    step_rows = min(512, length)
    key_heads = keys.reshape(length, heads_here, HDIM)
    value_heads = values.reshape(length, heads_here, HDIM)
    query_blocks = queries.reshape(length // step_rows, step_rows, heads_here, HDIM)
    upstream_blocks = upstream.reshape(length // step_rows, step_rows, heads_here, HDIM)

    def one_block(running, block_pair):
        key_grad, value_grad = running
        query_block, upstream_block = block_pair
        probability = head_probs(query_block, key_heads, factor)
        weights = probability.astype(jnp.bfloat16)
        value_grad = value_grad + jnp.einsum(
            "hqk,qhd->khd", weights, upstream_block, preferred_element_type=jnp.float32
        )
        prob_grad = jnp.einsum(
            "qhd,khd->hqk", upstream_block, value_heads, preferred_element_type=jnp.float32
        )
        center = jnp.sum(probability * prob_grad, axis=-1, keepdims=True)
        score_grad = (probability * (prob_grad - center)).astype(jnp.bfloat16)
        query_grad = (
            jnp.einsum("hqk,khd->qhd", score_grad, key_heads, preferred_element_type=jnp.float32)
            * factor
        )
        key_grad = (
            key_grad
            + jnp.einsum(
                "hqk,qhd->khd", score_grad, query_block, preferred_element_type=jnp.float32
            )
            * factor
        )
        return ((key_grad, value_grad), query_grad)

    empty_grad = jnp.zeros((length, heads_here, HDIM), jnp.float32)
    (key_grad, value_grad), query_grad = lax.scan(
        one_block, (empty_grad, empty_grad), (query_blocks, upstream_blocks)
    )
    return (
        query_grad.reshape(length, columns_all).astype(jnp.bfloat16),
        key_grad.reshape(length, columns_all).astype(jnp.bfloat16),
        value_grad.reshape(length, columns_all).astype(jnp.bfloat16),
    )


def body(
    teacher_query,
    teacher_key,
    teacher_value,
    hidden,
    adapter_down_weight,
    adapter_up_weight,
    guidance_index,
    timestep_index,
):
    cfg_index = lax.axis_index("cfg")
    seq_count = lax.axis_size("seq")
    tok_here = hidden.shape[2]
    total_rows = 2 * lax.axis_size("dp") * tok_here * seq_count
    input_features = hidden[0, 0]
    half_cols = input_features.shape[1] // (2 * seq_count)
    split_view = input_features.reshape(tok_here, 2, seq_count, half_cols)
    column_block = lax.all_to_all(split_view, "seq", split_axis=2, concat_axis=0, tiled=True)
    column_block = column_block.reshape(tok_here * seq_count, 2 * half_cols)
    own_pass = (teacher_query[0, :, 0], teacher_key[0, :, 0], teacher_value[0, :, 0])
    teacher_heads = (
        lax.all_to_all(own_pass[0], "seq", split_axis=2, concat_axis=1, tiled=True),
        lax.all_to_all(own_pass[1], "seq", split_axis=2, concat_axis=1, tiled=True),
        lax.all_to_all(own_pass[2], "seq", split_axis=2, concat_axis=1, tiled=True),
    )
    teacher_local = jnp.stack(
        [
            attention_forward(
                teacher_heads[0][half_index],
                teacher_heads[1][half_index],
                teacher_heads[2][half_index],
            )
            for half_index in range(2)
        ]
    )
    teacher_tokens = lax.all_to_all(
        teacher_local.astype(jnp.bfloat16), "seq", split_axis=1, concat_axis=2, tiled=True
    )
    guide_scale = 1.0 + 0.5 * guidance_index[:, 0].astype(jnp.float32)
    time_frac = (timestep_index[:, 0].astype(jnp.float32) + 0.5) / TSTEPS
    own_scale = lax.dynamic_index_in_dim(guide_scale, cfg_index, 0, keepdims=False)
    own_time = lax.dynamic_index_in_dim(time_frac, cfg_index, 0, keepdims=False)
    weighting = jnp.where(cfg_index == 0, guide_scale, 1.0 - guide_scale)
    weighted = weighting[:, None, None] * teacher_tokens.astype(jnp.float32)
    target = lax.psum_scatter(
        weighted.astype(jnp.bfloat16), "cfg", scatter_dimension=0, tiled=True
    ).astype(jnp.float32)[0]
    rank_index = jnp.arange(1, ADAPTER_RANK + 1).astype(jnp.float32)
    feature_modulation = 1.0 + 0.5 * jnp.cos(
        math.pi * rank_index * own_time + 0.25 * rank_index * own_scale
    )
    rank_projected = (
        jnp.einsum(
            "cl,elj->ecj", input_features, adapter_down_weight, preferred_element_type=jnp.float32
        )
        * feature_modulation
    ).astype(jnp.bfloat16)
    partner = passed_along(
        (teacher_query[0, 1, 0], teacher_key[0, 1, 0], teacher_value[0, 1, 0]), "cfg", 1
    )
    projected = []
    for stack_member in range(3):
        frozen = jnp.where(cfg_index == 0, own_pass[stack_member][0], partner[stack_member])
        adapted_output = jnp.dot(
            rank_projected[stack_member],
            adapter_up_weight[stack_member],
            preferred_element_type=jnp.float32,
        )
        projected.append((frozen.astype(jnp.float32) + adapted_output).astype(jnp.bfloat16))
    student = (
        lax.all_to_all(projected[0], "seq", split_axis=1, concat_axis=0, tiled=True),
        lax.all_to_all(projected[1], "seq", split_axis=1, concat_axis=0, tiled=True),
        lax.all_to_all(projected[2], "seq", split_axis=1, concat_axis=0, tiled=True),
    )
    student_local = attention_forward(student[0], student[1], student[2]).astype(jnp.bfloat16)
    student_tokens = lax.all_to_all(student_local, "seq", split_axis=0, concat_axis=1, tiled=True)
    upstream = (
        (student_tokens.astype(jnp.float32) - target) * (1.0 / math.sqrt(total_rows))
    ).astype(jnp.bfloat16)
    upstream_heads = lax.all_to_all(upstream, "seq", split_axis=1, concat_axis=0, tiled=True)
    grads_heads = attention_backward(student[0], student[1], student[2], upstream_heads)
    grads_tokens = (
        lax.all_to_all(grads_heads[0], "seq", split_axis=0, concat_axis=1, tiled=True),
        lax.all_to_all(grads_heads[1], "seq", split_axis=0, concat_axis=1, tiled=True),
        lax.all_to_all(grads_heads[2], "seq", split_axis=0, concat_axis=1, tiled=True),
    )
    gradient_stack = jnp.stack(grads_tokens)
    rank_backward = jnp.einsum(
        "sli,smi->slm", gradient_stack, adapter_up_weight, preferred_element_type=jnp.float32
    )
    up_partial = jnp.einsum(
        "ktr,ktc->krc", rank_projected, gradient_stack, preferred_element_type=jnp.float32
    )
    per_seq = lax.psum_scatter(
        up_partial.astype(jnp.bfloat16), "seq", scatter_dimension=2, tiled=True
    )
    grad_up = lax.psum_scatter(per_seq, ("cfg", "dp"), scatter_dimension=1, tiled=True).astype(
        jnp.float32
    )
    low_grad = (rank_backward * feature_modulation).astype(jnp.bfloat16)
    grad_rows = lax.all_gather(low_grad, "seq", axis=1, tiled=True)
    column_partial = jnp.einsum(
        "tc,ktr->kcr", column_block, grad_rows, preferred_element_type=jnp.float32
    )
    grad_down = lax.psum_scatter(
        column_partial.astype(jnp.bfloat16), ("cfg", "dp"), scatter_dimension=1, tiled=True
    ).astype(jnp.float32)
    return (student_tokens[None, None], grad_down, grad_up)


def solution(mesh):
    placed = (
        P("cfg", None, "dp", "seq", None),
        P("cfg", None, "dp", "seq", None),
        P("cfg", None, "dp", "seq", None),
        P("cfg", "dp", "seq", None),
        P(),
        P(),
        P(None, "dp"),
        P(None, "dp"),
    )
    return jax.shard_map(
        body,
        mesh=mesh,
        in_specs=placed,
        out_specs=(
            P("cfg", "dp", "seq", None),
            P(None, ("cfg", "seq", "dp"), None),
            P(None, ("cfg", "dp"), "seq"),
        ),
        check_vma=False,
    )
```

profile of v0, /device:TPU:0, one launch (start us, length us, event | category | flops | bytes accessed | tf_op | source)
XLA Modules:
  0.0 490.0 jit_solution(14562616477603965680)
XLA Ops:
  7.2 3.8 copy.104
  11.0 7.3 %all-to-all-start.5 = ((bf16[2,128,2048]{1,0,2:T(2,128)(2,1)}), bf16[2,128,2048]{1,0,2:T(2,128)(2,1)}, u32[]{:S(2)}, u32[]{:S(2)}) async-start(bf16[2,128,2048]{1,0,2:T(2,128)(2,1)} %bitcast.305), calls=%async_computation.5 | async-start | bytes 2097152 | tf_op jit(solution)/shard_map/all_to_all | solution.py:114
  18.3 3.6 copy.106
  22.0 22.2 %all-to-all-done.5 = bf16[2,128,2048]{1,0,2:T(2,128)(2,1)} async-done(((bf16[2,128,2048]{1,0,2:T(2,128)(2,1)}), bf16[2,128,2048]{1,0,2:T(2,128)(2,1)}, u32[]{:S(2)}, u32[]{:S(2)}) %all-to-all-start.5) | async-done | bytes 1048608 | tf_op jit(solution)/shard_map/all_to_all | solution.py:114
  44.2 4.2 all-to-all-start.6
  49.3 4.2 collective-permute-start.1
  53.5 1.9 slice_bitcast_fusion
  55.4 2.1 collective-permute-start.2
  57.5 3.7 copy.102
  61.2 12.8 %all-to-all-done.6 = bf16[2,128,2048]{1,0,2:T(2,128)(2,1)} async-done(((bf16[2,128,2048]{1,0,2:T(2,128)(2,1)}), bf16[2,128,2048]{1,0,2:T(2,128)(2,1)}, u32[]{:S(2)}, u32[]{:S(2)}) %all-to-all-start.6) | async-done | bytes 1048608 | tf_op jit(solution)/shard_map/all_to_all | solution.py:115
  74.0 4.3 all-to-all-start.4
  78.3 1.9 slice_bitcast_fusion.2
  80.2 4.2 collective-permute-start
  86.4 2.0 fusion.91
  92.4 11.4 %all-to-all-done.4 = bf16[2,128,2048]{1,0,2:T(2,128)(2,1)} async-done(((bf16[2,128,2048]{1,0,2:T(2,128)(2,1)}), bf16[2,128,2048]{1,0,2:T(2,128)(2,1)}, u32[]{:S(2)}, u32[]{:S(2)}) %all-to-all-start.4) | async-done | bytes 1048608 | tf_op jit(solution)/shard_map/all_to_all | solution.py:113
  103.7 3.5 all-to-all-start.1
  110.5 1.9 copy.188
  113.7 1.9 copy.187
  117.7 2.4 copy.103
  121.8 5.4 %all-to-all-start.2 = ((bf16[128,8,256]{0,2,1:T(8,128)(2,1)}), bf16[128,8,256]{0,2,1:T(8,128)(2,1)S(1)}, u32[]{:S(2)}, u32[]{:S(2)}) async-start(bf16[128,8,256]{0,2,1:T(8,128)(2,1)} %bitcast.28), calls=%async_computation.2 | async-start | bytes 1048576 | tf_op jit(solution)/shard_map/all_to_all | solution.py:164
  127.2 15.5 %while.46 = (s32[]{:T(128)}, bf16[2,512,2,128]{3,1,2,0:T(8,128)(2,1)S(1)}, bf16[2,512,2,128]{3,2,1,0:T(2,128)(2,1)S(1)}, bf16[1024,2,128]{2,0,1:T(8,128)(2,1)}, bf16[1024,2,128]{2,0,1:T(8,128)(2,1)}, /*index=5*/s32[]{:T(128)}) while((s32[]{:T(128)}, bf16[2,512,2,128]{3,1,2,0:T(8,128)(2,1)S(1)}, bf16[2,512,2,128]{3,2,1,0:T(2,128)(2,1)S(1)}, ...), condition=%wide.region_7.8_spmd, body=%wide.region_4.7_spmd.sunk | while | flops 542114816 | bytes 10756173 | solution.py:42
  127.4 4.4 fusion.182
  131.8 3.1 fusion.183
  135.2 4.4 fusion.182
  139.6 3.1 fusion.183
  147.4 6.0 %all-to-all-start = ((bf16[128,8,256]{2,0,1:T(8,128)(2,1)}), bf16[128,8,256]{2,0,1:T(8,128)(2,1)S(1)}, u32[]{:S(2)}, u32[]{:S(2)}) async-start(bf16[128,8,256]{2,0,1:T(8,128)(2,1)} %bitcast.251), calls=%async_computation | async-start | bytes 1048576 | tf_op jit(solution)/shard_map/all_to_all | solution.py:162
  154.3 16.8 %while.47 = (s32[]{:T(128)}, bf16[2,512,2,128]{3,1,2,0:T(8,128)(2,1)}, bf16[2,512,2,128]{3,2,1,0:T(2,128)(2,1)S(1)}, bf16[1024,2,128]{2,0,1:T(8,128)(2,1)}, bf16[1024,2,128]{2,0,1:T(8,128)(2,1)}, /*index=5*/s32[]{:T(128)}) while((s32[]{:T(128)}, bf16[2,512,2,128]{3,1,2,0:T(8,128)(2,1)}, bf16[2,512,2,128]{3,2,1,0:T(2,128)(2,1)S(1)}, ...), condition=%wide.region_11.12_spmd, body=%wide.region_8.11_spmd.sunk | while | flops 542114816 | bytes 10756681 | solution.py:42
  154.4 4.4 fusion.186
  158.8 3.8 fusion.187
  162.8 4.4 fusion.186
  167.2 3.8 fusion.187
  176.7 2.0 copy.116
  179.5 6.0 %all-to-all-start.7 = ((bf16[2,1024,256]{2,0,1:T(2,128)(2,1)}), bf16[2,1024,256]{2,0,1:T(2,128)(2,1)S(1)}, u32[]{:S(2)}, u32[]{:S(2)}) async-start(bf16[2,1024,256]{2,0,1:T(2,128)(2,1)} %copy.116), calls=%async_computation.7 | async-start | bytes 2097152 | tf_op jit(solution)/shard_map/all_to_all | solution.py:127
  189.0 21.0 %all-to-all-done.7 = bf16[2,1024,256]{2,0,1:T(2,128)(2,1)S(1)} async-done(((bf16[2,1024,256]{2,0,1:T(2,128)(2,1)}), bf16[2,1024,256]{2,0,1:T(2,128)(2,1)S(1)}, u32[]{:S(2)}, u32[]{:S(2)}) %all-to-all-start.7) | async-done | bytes 1048608 | tf_op jit(solution)/shard_map/all_to_all | solution.py:127
  211.7 2.0 copy.118
  215.0 13.1 %while.45 = (s32[]{:T(128)}, bf16[2,512,2,128]{3,1,2,0:T(8,128)(2,1)S(1)}, bf16[2,512,2,128]{3,1,2,0:T(8,128)(2,1)S(1)}, bf16[1024,2,128]{2,0,1:T(8,128)(2,1)S(1)}, bf16[1024,2,128]{2,0,1:T(8,128)(2,1)}, /*index=5*/s32[]{:T(128)}) while((s32[]{:T(128)}, bf16[2,512,2,128]{3,1,2,0:T(8,128)(2,1)S(1)}, bf16[2,512,2,128]{3,1,2,0:T(8,128)(2,1)S(1)}, ...), condition=%wide.region_3.4_spmd, body=%wide.region_0.3_spmd.sunk | while | flops 542114816 | bytes 12329065 | solution.py:42
  215.1 3.3 fusion.178
  218.4 3.3 fusion.179
  221.8 3.3 fusion.178
  225.1 3.0 fusion.179
  229.9 3.5 all-to-all-start.3
  235.7 11.8 %all-to-all-done.3 = bf16[8,128,256]{2,1,0:T(8,128)(2,1)S(1)} async-done(((bf16[8,128,256]{2,1,0:T(8,128)(2,1)}), bf16[8,128,256]{2,1,0:T(8,128)(2,1)S(1)}, u32[]{:S(2)}, u32[]{:S(2)}) %all-to-all-start.3) | async-done | bytes 524320 | tf_op jit(solution)/shard_map/all_to_all | solution.py:167
  248.5 3.7 all-to-all-start.8
  252.3 14.4 %all-to-all-done.8 = bf16[128,8,256]{2,0,1:T(8,128)(2,1)S(1)} async-done(((bf16[128,8,256]{2,0,1:T(8,128)(2,1)}), bf16[128,8,256]{2,0,1:T(8,128)(2,1)S(1)}, u32[]{:S(2)}, u32[]{:S(2)}) %all-to-all-start.8) | async-done | bytes 524320 | tf_op jit(solution)/shard_map/all_to_all | solution.py:171
  267.7 31.3 %while.48 = (s32[]{:T(128)}, f32[1024,2,128]{0,2,1:T(8,128)S(1)}, f32[1024,2,128]{0,2,1:T(8,128)}, bf16[2,512,2,128]{3,1,2,0:T(8,128)(2,1)}, bf16[2,512,2,128]{3...) while((s32[]{:T(128)}, f32[1024,2,128]{0,2,1:T(8,128)S(1)}, ...), condition=%wide.region_17.18_spmd.clone, body=%wide.region_13.17_spmd.clone.sunk | while | flops 1356201984 | bytes 79193864 | solution.py:82
  267.7 4.6 fusion.196
  272.6 3.1 multiply_reduce_fusion.6
  278.4 2.5 fusion.199
  282.7 4.7 fusion.196
  287.5 3.1 multiply_reduce_fusion.6
  293.4 2.5 fusion.199
  295.9 3.1 fusion.198
  301.7 3.6 all-to-all-start.9
  306.7 13.4 %all-to-all-done.9 = bf16[8,128,256]{2,1,0:T(8,128)(2,1)S(1)} async-done(((bf16[8,128,256]{2,1,0:T(8,128)(2,1)}), bf16[8,128,256]{2,1,0:T(8,128)(2,1)S(1)}, u32[]{:S(2)}, u32[]{:S(2)}) %all-to-all-start.9) | async-done | bytes 524320 | tf_op jit(solution)/shard_map/all_to_all | solution.py:174
  320.0 3.6 all-to-all-start.10
  326.2 12.1 %all-to-all-done.10 = bf16[8,128,256]{2,1,0:T(8,128)(2,1)S(1)} async-done(((bf16[8,128,256]{2,1,0:T(8,128)(2,1)}), bf16[8,128,256]{2,1,0:T(8,128)(2,1)S(1)}, u32[]{:S(2)}, u32[]{:S(2)}) %all-to-all-start.10) | async-done | bytes 524320 | tf_op jit(solution)/shard_map/all_to_all | solution.py:175
  338.3 3.6 all-to-all-start.11
  343.2 13.5 %all-to-all-done.11 = bf16[8,128,256]{2,1,0:T(8,128)(2,1)S(1)} async-done(((bf16[8,128,256]{2,1,0:T(8,128)(2,1)}), bf16[8,128,256]{2,1,0:T(8,128)(2,1)S(1)}, u32[]{:S(2)}, u32[]{:S(2)}) %all-to-all-start.11) | async-done | bytes 524320 | tf_op jit(solution)/shard_map/all_to_all | solution.py:176
  362.6 36.0 %all_to_all.182 = bf16[128,2,8,192]{0,3,1,2:T(8,128)(2,1)S(1)} all-to-all(bf16[128,2,8,192]{0,3,1,2:T(8,128)(2,1)S(1)} %copy.131), channel_id=1, replica_groups=mesh['cfg'=2,'seq'=8,'dp'=2] {'seq'}, dimensions={2} | all-to-all | bytes 1572864 | tf_op jit(solution)/shard_map/all_to_all | solution.py:109
  400.3 2.6 fusion.92
  402.9 32.7 %all_gather.3 = bf16[3,1024,128]{2,1,0:T(8,128)(2,1)S(1)} all-gather(bf16[3,128,128]{2,1,0:T(8,128)(2,1)S(1)} %fusion.92), channel_id=1, replica_groups=mesh['cfg'=2,'seq'=8,'dp'=2] {'seq'}, dimensions={1}, use_global_device_ids=true | all-gather | bytes 884736 | tf_op jit(solution)/shard_map/all_gather | solution.py:192
  435.7 2.5 fusion.90
  442.0 17.9 %reduce-scatter.13.cloned.1.call-done = bf16[96,384]{1,0:T(8,128)(2,1)} async-done(((bf16[384,384]{1,0:T(8,128)(2,1)}), bf16[96,384]{1,0:T(8,128)(2,1)}) %reduce-scatter.13.cloned.1.call-update) | async-done | bytes 73744
  461.7 20.3 %reduce-scatter.11.cloned.1.call-done = bf16[3,32,256]{2,1,0:T(8,128)(2,1)} async-done(((bf16[3,128,256]{2,1,0:T(8,128)(2,1)}), bf16[3,32,256]{2,1,0:T(8,128)(2,1)}) %reduce-scatter.11.cloned.1.call-update) | async-done | bytes 49168 | tf_op jit(solution)/shard_map/reduce_scatter | solution.py:188
  (171 shorter events, 69.0 us)
Async XLA Ops:
  7.2 79.2 %copy-start = (bf16[3,3072,128]{2,1,0:T(8,128)(2,1)S(1)}, bf16[3,3072,128]{2,1,0:T(8,128)(2,1)}, u32[]{:S(2)}) copy-start(bf16[3,3072,128]{2,1,0:T(8,128)(2,1)} %param.20) | copy-start | bytes 7077892
  7.2 41.3 %copy-start.10 = (bf16[1,2,1,128,2048]{4,3,2,1,0:T(8,128)(2,1)S(1)}, bf16[1,2,1,128,2048]{4,3,2,1,0:T(8,128)(2,1)}, u32[]{:S(2)}) copy-start(bf16[1,2,1,128,2048]{4,3,2,1,0:T(8,128)(2,1)} %param.17) | copy-start | bytes 3145732
  11.0 33.2 %all-to-all-start.5 = ((bf16[2,128,2048]{1,0,2:T(2,128)(2,1)}), bf16[2,128,2048]{1,0,2:T(2,128)(2,1)}, u32[]{:S(2)}, u32[]{:S(2)}) async-start(bf16[2,128,2048]{1,0,2:T(2,128)(2,1)} %bitcast.305), calls=%async_computation.5 | async-start | bytes 2097152 | tf_op jit(solution)/shard_map/all_to_all | solution.py:114
  44.2 29.8 %all-to-all-start.6 = ((bf16[2,128,2048]{1,0,2:T(2,128)(2,1)}), bf16[2,128,2048]{1,0,2:T(2,128)(2,1)}, u32[]{:S(2)}, u32[]{:S(2)}) async-start(bf16[2,128,2048]{1,0,2:T(2,128)(2,1)} %bitcast.304), calls=%async_computation.6 | async-start | bytes 2097152 | tf_op jit(solution)/shard_map/all_to_all | solution.py:115
  48.5 35.9 %copy-start.23 = (s32[2,1]{0,1:T(1,128)S(1)}, s32[2,1]{0,1:T(1,128)}, u32[]{:S(2)}) copy-start(s32[2,1]{0,1:T(1,128)} %param.23) | copy-start | bytes 28
  48.5 35.9 %copy-start.24 = (s32[2,1]{0,1:T(1,128)S(1)}, s32[2,1]{0,1:T(1,128)}, u32[]{:S(2)}) copy-start(s32[2,1]{0,1:T(1,128)} %param.22) | copy-start | bytes 28
  49.3 39.0 %collective-permute-start.1 = (bf16[128,2048]{1,0:T(8,128)(2,1)}, bf16[128,2048]{1,0:T(8,128)(2,1)}, u32[]{:S(2)}, u32[]{:S(2)}) collective-permute-start(bf16[128,2048]{1,0:T(8,128)(2,1)} %slice_bitcast_fusion.1), channel_id=1, source_target_pairs={{0,16},{1,17},{2,18},{3,19},{4,20},{5,21},{6,22},{7,23},{8,24},{9,... | collective-permute-start | bytes 1572872 | tf_op jit(solution)/shard_map/ppermute | solution.py:16
  55.4 35.4 %collective-permute-start.2 = (bf16[128,2048]{1,0:T(8,128)(2,1)}, bf16[128,2048]{1,0:T(8,128)(2,1)}, u32[]{:S(2)}, u32[]{:S(2)}) collective-permute-start(bf16[128,2048]{1,0:T(8,128)(2,1)} %slice_bitcast_fusion), channel_id=1, source_target_pairs={{0,16},{1,17},{2,18},{3,19},{4,20},{5,21},{6,22},{7,23},{8,24},{9,... | collective-permute-start | bytes 1572872 | tf_op jit(solution)/shard_map/ppermute | solution.py:16
  74.0 29.7 %all-to-all-start.4 = ((bf16[2,128,2048]{1,0,2:T(2,128)(2,1)}), bf16[2,128,2048]{1,0,2:T(2,128)(2,1)}, u32[]{:S(2)}, u32[]{:S(2)}) async-start(bf16[2,128,2048]{1,0,2:T(2,128)(2,1)} %bitcast.303), calls=%async_computation.4 | async-start | bytes 2097152 | tf_op jit(solution)/shard_map/all_to_all | solution.py:113
  80.2 27.0 %collective-permute-start = (bf16[128,2048]{1,0:T(8,128)(2,1)}, bf16[128,2048]{1,0:T(8,128)(2,1)}, u32[]{:S(2)}, u32[]{:S(2)}) collective-permute-start(bf16[128,2048]{1,0:T(8,128)(2,1)} %slice_bitcast_fusion.2), channel_id=1, source_target_pairs={{0,16},{1,17},{2,18},{3,19},{4,20},{5,21},{6,22},{7,23},{8,24},{9,... | collective-permute-start | bytes 1572872 | tf_op jit(solution)/shard_map/ppermute | solution.py:16
  86.4 2.0 copy-start.21
  88.3 20.3 %copy-start.15 = (bf16[3,128,128]{2,1,0:T(8,128)(2,1)}, bf16[3,128,128]{2,1,0:T(8,128)(2,1)S(1)}, u32[]{:S(2)}) copy-start(bf16[3,128,128]{2,1,0:T(8,128)(2,1)S(1)} %fusion.91) | copy-start | bytes 294916
  88.3 18.9 %copy-start.11 = (bf16[1,2,1,128,2048]{4,3,2,1,0:T(8,128)(2,1)S(1)}, bf16[1,2,1,128,2048]{4,3,2,1,0:T(8,128)(2,1)}, u32[]{:S(2)}) copy-start(bf16[1,2,1,128,2048]{4,3,2,1,0:T(8,128)(2,1)} %param.16) | copy-start | bytes 3145732
  103.7 18.0 %all-to-all-start.1 = ((bf16[128,8,256]{0,2,1:T(8,128)(2,1)}), bf16[128,8,256]{0,2,1:T(8,128)(2,1)S(1)}, u32[]{:S(2)}, u32[]{:S(2)}) async-start(bf16[128,8,256]{0,2,1:T(8,128)(2,1)} %bitcast.22), calls=%async_computation.1 | async-start | bytes 1048576 | tf_op jit(solution)/shard_map/all_to_all | solution.py:163
  121.8 25.6 %all-to-all-start.2 = ((bf16[128,8,256]{0,2,1:T(8,128)(2,1)}), bf16[128,8,256]{0,2,1:T(8,128)(2,1)S(1)}, u32[]{:S(2)}, u32[]{:S(2)}) async-start(bf16[128,8,256]{0,2,1:T(8,128)(2,1)} %bitcast.28), calls=%async_computation.2 | async-start | bytes 1048576 | tf_op jit(solution)/shard_map/all_to_all | solution.py:164
  147.4 31.4 %all-to-all-start = ((bf16[128,8,256]{2,0,1:T(8,128)(2,1)}), bf16[128,8,256]{2,0,1:T(8,128)(2,1)S(1)}, u32[]{:S(2)}, u32[]{:S(2)}) async-start(bf16[128,8,256]{2,0,1:T(8,128)(2,1)} %bitcast.251), calls=%async_computation | async-start | bytes 1048576 | tf_op jit(solution)/shard_map/all_to_all | solution.py:162
  178.7 0.8 copy-start.13
  179.5 30.4 %all-to-all-start.7 = ((bf16[2,1024,256]{2,0,1:T(2,128)(2,1)}), bf16[2,1024,256]{2,0,1:T(2,128)(2,1)S(1)}, u32[]{:S(2)}, u32[]{:S(2)}) async-start(bf16[2,1024,256]{2,0,1:T(2,128)(2,1)} %copy.116), calls=%async_computation.7 | async-start | bytes 2097152 | tf_op jit(solution)/shard_map/all_to_all | solution.py:127
  185.5 3.3 copy-start.14
  185.5 48.9 %reduce-scatter.7.cloned.1.call-start = ((), (), s32[]{:S(2)}) async-start(), calls=%async_computation.17 | async-start | bytes 1572864 | tf_op jit(solution)/shard_map/reduce_scatter | solution.py:136
  211.7 3.3 copy-start.17
  215.1 3.4 copy-start.18
  221.8 3.4 copy-start.18
  228.2 20.3 %copy-start.5 = (bf16[2,512,2,128]{3,1,2,0:T(8,128)(2,1)}, bf16[2,512,2,128]{3,1,2,0:T(8,128)(2,1)S(1)}, u32[]{:S(2)}) copy-start(bf16[2,512,2,128]{3,1,2,0:T(8,128)(2,1)S(1)} %get-tuple-element.556) | copy-start | bytes 1572868
  228.7 39.0 %copy-start.19 = (bf16[1024,2,128]{2,0,1:T(8,128)(2,1)S(1)}, bf16[1024,2,128]{2,0,1:T(8,128)(2,1)}, u32[]{:S(2)}) copy-start(bf16[1024,2,128]{2,0,1:T(8,128)(2,1)} %get-tuple-element.580) | copy-start | bytes 1572868
  229.9 17.7 %all-to-all-start.3 = ((bf16[8,128,256]{2,1,0:T(8,128)(2,1)}), bf16[8,128,256]{2,1,0:T(8,128)(2,1)S(1)}, u32[]{:S(2)}, u32[]{:S(2)}) async-start(bf16[8,128,256]{2,1,0:T(8,128)(2,1)} %convert_element_type.143), calls=%async_computation.3 | async-start | bytes 1048576 | tf_op jit(solution)/shard_map/all_to_all | solution.py:167
  247.5 19.1 %copy-start.8 = (bf16[8,128,256]{2,1,0:T(8,128)(2,1)}, bf16[8,128,256]{2,1,0:T(8,128)(2,1)S(1)}, u32[]{:S(2)}) copy-start(bf16[8,128,256]{2,1,0:T(8,128)(2,1)S(1)} %all-to-all-done.3) | copy-start | bytes 1572868
  248.5 18.1 %all-to-all-start.8 = ((bf16[128,8,256]{2,0,1:T(8,128)(2,1)}), bf16[128,8,256]{2,0,1:T(8,128)(2,1)S(1)}, u32[]{:S(2)}, u32[]{:S(2)}) async-start(bf16[128,8,256]{2,0,1:T(8,128)(2,1)} %multiply_convert_fusion.1), calls=%async_computation.9 | async-start | bytes 1048576 | tf_op jit(solution)/shard_map/all_to_all | solution.py:171
  267.7 8.0 %copy-start.6 = (bf16[2,512,2,128]{3,2,1,0:T(2,128)(2,1)}, bf16[2,512,2,128]{3,2,1,0:T(2,128)(2,1)S(1)}, u32[]{:S(2)}) copy-start(bf16[2,512,2,128]{3,2,1,0:T(2,128)(2,1)S(1)} %get-tuple-element.548) | copy-start | bytes 1572868 | tf_op jit(solution)/shard_map/while
  272.5 3.5 copy-start.2
  276.7 4.2 copy-start.3
  280.9 1.8 copy-start.7
  280.9 1.8 copy-start.20
  282.7 8.0 %copy-start.6 = (bf16[2,512,2,128]{3,2,1,0:T(2,128)(2,1)}, bf16[2,512,2,128]{3,2,1,0:T(2,128)(2,1)S(1)}, u32[]{:S(2)}) copy-start(bf16[2,512,2,128]{3,2,1,0:T(2,128)(2,1)S(1)} %get-tuple-element.548) | copy-start | bytes 1572868 | tf_op jit(solution)/shard_map/while
  287.5 3.5 copy-start.2
  291.6 4.3 copy-start.3
  295.9 3.1 copy-start.7
  295.9 3.1 copy-start.20
  301.7 18.3 %all-to-all-start.9 = ((bf16[8,128,256]{2,1,0:T(8,128)(2,1)}), bf16[8,128,256]{2,1,0:T(8,128)(2,1)S(1)}, u32[]{:S(2)}, u32[]{:S(2)}) async-start(bf16[8,128,256]{2,1,0:T(8,128)(2,1)} %convert_element_type.152), calls=%async_computation.10 | async-start | bytes 1048576 | tf_op jit(solution)/shard_map/all_to_all | solution.py:174
  320.0 18.3 %all-to-all-start.10 = ((bf16[8,128,256]{2,1,0:T(8,128)(2,1)}), bf16[8,128,256]{2,1,0:T(8,128)(2,1)S(1)}, u32[]{:S(2)}, u32[]{:S(2)}) async-start(bf16[8,128,256]{2,1,0:T(8,128)(2,1)} %copy.144), calls=%async_computation.11 | async-start | bytes 1048576 | tf_op jit(solution)/shard_map/all_to_all | solution.py:175
  338.3 18.3 %all-to-all-start.11 = ((bf16[8,128,256]{2,1,0:T(8,128)(2,1)}), bf16[8,128,256]{2,1,0:T(8,128)(2,1)S(1)}, u32[]{:S(2)}, u32[]{:S(2)}) async-start(bf16[8,128,256]{2,1,0:T(8,128)(2,1)} %copy.145), calls=%async_computation.12 | async-start | bytes 1048576 | tf_op jit(solution)/shard_map/all_to_all | solution.py:176
  342.0 98.2 %reduce-scatter.9.cloned.1.call-start = ((), (), s32[]{:S(2)}) async-start(), calls=%async_computation.18 | async-start | bytes 1769472 | tf_op jit(solution)/shard_map/reduce_scatter | solution.py:185
  342.3 18.0 %copy-start.16 = (bf16[3,128,128]{2,1,0:T(8,128)(2,1)S(1)}, bf16[3,128,128]{2,1,0:T(8,128)(2,1)}, u32[]{:S(2)}) copy-start(bf16[3,128,128]{2,1,0:T(8,128)(2,1)} %copy-done.15) | copy-start | bytes 294916
  357.7 4.5 copy-start.12
  359.2 1.2 copy-start.4
  362.1 38.2 %copy-start.22 = (f32[128]{0:T(128)S(1)}, f32[128]{0:T(128)}, u32[]{:S(2)}) copy-start(f32[128]{0:T(128)} %copy-done.21) | copy-start | bytes 1540
  362.1 97.8 %reduce-scatter.13.cloned.1.call-start = ((), (), s32[]{:S(2)}) async-start(), calls=%async_computation.20 | async-start | bytes 368640
  400.3 40.4 %copy-start.9 = (bf16[8,128,256]{2,1,0:T(8,128)(2,1)S(1)}, bf16[8,128,256]{2,1,0:T(8,128)(2,1)}, u32[]{:S(2)}) copy-start(bf16[8,128,256]{2,1,0:T(8,128)(2,1)} %copy-done.8) | copy-start | bytes 1572868
  400.3 83.1 %copy-start.1 = (bf16[3,3072,128]{2,1,0:T(8,128)(2,1)S(1)}, bf16[3,3072,128]{2,1,0:T(8,128)(2,1)}, u32[]{:S(2)}) copy-start(bf16[3,3072,128]{2,1,0:T(8,128)(2,1)} %param.20) | copy-start | bytes 7077892
  440.1 41.9 %reduce-scatter.11.cloned.1.call-start = ((), (), s32[]{:S(2)}) async-start(), calls=%async_computation.19 | async-start | bytes 245760 | tf_op jit(solution)/shard_map/reduce_scatter | solution.py:188
Sparse Core Ops, SparseCore 0:
  215.1 19.3 reduce-scatter.6
  362.2 74.5 reduce-scatter.8
  440.2 19.5 reduce-scatter.12
  462.2 19.7 reduce-scatter.10
where the time goes:
time: 493 us; the launch traced here: 490 us
  waiting for transfers between devices  173 us (35%)
  matrix products  86.5 us (18%)
  local copies, waits for them, and re-layouts  70.6 us (14%)
  blocking collectives  68.7 us (14%)
  starting transfers between devices  65.5 us (13%)
  between operations  15.7 us (3%)
  other arithmetic  9.88 us (2%)
    all_to_all x1, blocking collectives, body(): lax.all_to_all(split_view, 'seq', split_axis=2, concat_axis=0, tiled=True)  36 us
    sub x8, matrix products, head_probs(): raised = jnp.exp(scores - highest)  33.6 us
    all_gather x1, blocking collectives, body(): grad_rows = lax.all_gather(low_grad, 'seq', axis=1, tiled=True)  32.7 us
    all_to_all x1, waiting for transfers between devices, body(): lax.all_to_all(own_pass[1], 'seq', split_axis=2, concat_axis=1, tiled=True)  22.2 us
    all_to_all x1, waiting for transfers between devices, body(): lax.all_to_all(teacher_local.astype(jnp.bfloat16), 'seq', split_axis=1, c...  21 us
    reduce_scatter x1, waiting for transfers between devices, body(): lax.psum_scatter(per_seq, ('cfg', 'dp'), scatter_dimension=1, tiled=True)  20.3 us
    dot_general x6, matrix products, one_block(): jnp.einsum('hqk,khd->qhd', weights, value_heads, preferred_element_type=j...  20.2 us
    unnamed x52, local copies, waits for them, and re-layouts  18.6 us
  transfers between devices with their start and end apart: 19, of which 13 were waited for; matrix products, arithmetic and copies ran while one was open for 23% of the time, Pallas kernels for 0%

commit v1 on v0

v1 whole, which is shorter than its diff:
```python
import functools
import math

import jax
import jax.numpy as jnp
from jax import lax
from jax.experimental import pallas as pl
from jax.experimental.pallas import tpu as pltpu
from jax.sharding import PartitionSpec as P

HDIM = 128
ADAPTER_RANK = 128
TSTEPS = 1000
FACTOR = HDIM ** (-0.5)
FACTOR_BASE2 = FACTOR * math.log2(math.e)
VMEM_LIMIT = 48 * 1024 * 1024

NT = (((1,), (1,)), ((), ()))
TN = (((0,), (0,)), ((), ()))


def dot_f32(left, right):
    return jnp.dot(left, right, preferred_element_type=jnp.float32)


def dot_nt(left, right):
    return lax.dot_general(left, right, NT, preferred_element_type=jnp.float32)


def probs_by_key(key_head, query_block):
    scores = dot_nt(key_head, query_block)
    highest = jnp.max(scores, axis=0, keepdims=True)
    raised = jnp.exp2((scores - highest) * FACTOR_BASE2)
    return raised * (1.0 / jnp.sum(raised, axis=0, keepdims=True))


def teacher_kernel(step_rows, half_ref, weight_ref, query_ref, key_ref, value_ref, out_ref, value_t):
    length = query_ref.shape[1]
    weight = weight_ref[0]
    value_t[...] = value_ref[0].T

    def one_block(step, _):
        rows = pl.ds(pl.multiple_of(step * step_rows, step_rows), step_rows)
        weights = probs_by_key(key_ref[0], query_ref[0, rows, :]).astype(jnp.bfloat16)
        attended = dot_f32(value_t[...], weights).T.astype(jnp.bfloat16)
        out_ref[rows, :] = (weight * attended.astype(jnp.float32)).astype(jnp.bfloat16)
        return 0

    lax.fori_loop(0, length // step_rows, one_block, 0)


def teacher_attention(half, weight, heads):
    _, length, columns = heads[0].shape
    heads_here = columns // HDIM
    step_rows = min(256, length)
    block = pl.BlockSpec((1, length, HDIM), lambda head, half_ref, weight_ref: (half_ref[0], 0, head))
    return pl.pallas_call(
        functools.partial(teacher_kernel, step_rows),
        out_shape=jax.ShapeDtypeStruct((length, columns), jnp.bfloat16),
        grid_spec=pltpu.PrefetchScalarGridSpec(
            num_scalar_prefetch=2,
            grid=(heads_here,),
            in_specs=[block, block, block],
            out_specs=pl.BlockSpec((length, HDIM), lambda head, half_ref, weight_ref: (0, head)),
            scratch_shapes=[pltpu.VMEM((HDIM, length), jnp.bfloat16)],
        ),
        compiler_params=pltpu.CompilerParams(
            dimension_semantics=("arbitrary",), vmem_limit_bytes=VMEM_LIMIT
        ),
        cost_estimate=pl.CostEstimate(
            flops=4 * heads_here * length * length * HDIM,
            bytes_accessed=8 * length * columns,
            transcendentals=heads_here * length * length,
        ),
        name="teacher",
    )(half[None], weight[None], *heads)


def student_kernel(
    step_rows,
    out_scale,
    cfg_ref,
    own_query,
    own_key,
    own_value,
    sent_query,
    sent_key,
    sent_value,
    rank_ref,
    up_ref,
    target_own,
    target_sent,
    out_ref,
    grad_up_ref,
    back_ref,
    s_query,
    s_key,
    s_value,
    key_t,
    value_t,
    grad_query,
    grad_key,
    grad_value,
    back_sum,
):
    length = rank_ref.shape[0]
    head = pl.program_id(0)
    first = cfg_ref[0] == 0

    for member, (own, sent, projected) in enumerate(
        ((own_query, sent_query, s_query), (own_key, sent_key, s_key), (own_value, sent_value, s_value))
    ):
        low_rank = rank_ref[:, member * ADAPTER_RANK : (member + 1) * ADAPTER_RANK]
        frozen = jnp.where(first, own[0].astype(jnp.float32), sent[...].astype(jnp.float32))
        projected[...] = (frozen + dot_f32(low_rank, up_ref[member])).astype(jnp.bfloat16)
    key_t[...] = s_key[...].T
    value_t[...] = s_value[...].T
    grad_key[...] = jnp.zeros_like(grad_key)
    grad_value[...] = jnp.zeros_like(grad_value)

    def one_block(step, _):
        rows = pl.ds(pl.multiple_of(step * step_rows, step_rows), step_rows)
        query_block = s_query[rows, :]
        probability = probs_by_key(s_key[...], query_block)
        weights = probability.astype(jnp.bfloat16)
        attended = dot_f32(value_t[...], weights).T.astype(jnp.bfloat16)
        out_ref[rows, :] = attended
        target = target_own[rows, :].astype(jnp.float32) + target_sent[rows, :].astype(jnp.float32)
        upstream = ((attended.astype(jnp.float32) - target) * out_scale).astype(jnp.bfloat16)
        grad_value[...] += dot_f32(weights, upstream)
        prob_grad = dot_nt(s_value[...], upstream)
        center = jnp.sum(probability * prob_grad, axis=0, keepdims=True)
        score_grad = (probability * (prob_grad - center)).astype(jnp.bfloat16)
        grad_key[...] += dot_f32(score_grad, query_block)
        grad_query[rows, :] = (dot_f32(key_t[...], score_grad).T * FACTOR).astype(jnp.bfloat16)
        return 0

    lax.fori_loop(0, length // step_rows, one_block, 0)

    gradients = (
        grad_query[...],
        (grad_key[...] * FACTOR).astype(jnp.bfloat16),
        grad_value[...].astype(jnp.bfloat16),
    )
    for member, gradient in enumerate(gradients):
        columns = slice(member * ADAPTER_RANK, (member + 1) * ADAPTER_RANK)
        grad_up_ref[member] = lax.dot_general(
            rank_ref[:, columns], gradient, TN, preferred_element_type=jnp.float32
        ).astype(jnp.bfloat16)
        back = dot_nt(gradient, up_ref[member])

        @pl.when(head == 0)
        def _():
            back_sum[:, columns] = back

        @pl.when(head > 0)
        def _():
            back_sum[:, columns] += back

    @pl.when(head == pl.num_programs(0) - 1)
    def _():
        back_ref[...] = back_sum[...].astype(jnp.bfloat16)


def student_step(cfg_index, total_rows, own, sent, rank_all, up_here, target_own, target_sent):
    length, columns = target_own.shape
    heads_here = columns // HDIM
    step_rows = min(256, length)
    ranks = rank_all.shape[1]
    own_block = pl.BlockSpec((1, length, HDIM), lambda head, cfg_ref: (0, 0, head))
    block = pl.BlockSpec((length, HDIM), lambda head, cfg_ref: (0, head))
    whole = pl.BlockSpec((length, ranks), lambda head, cfg_ref: (0, 0))
    up_block = pl.BlockSpec((3, ADAPTER_RANK, HDIM), lambda head, cfg_ref: (0, 0, head))
    return pl.pallas_call(
        functools.partial(student_kernel, step_rows, 1.0 / math.sqrt(total_rows)),
        out_shape=(
            jax.ShapeDtypeStruct((length, columns), jnp.bfloat16),
            jax.ShapeDtypeStruct((3, ADAPTER_RANK, columns), jnp.bfloat16),
            jax.ShapeDtypeStruct((length, ranks), jnp.bfloat16),
        ),
        grid_spec=pltpu.PrefetchScalarGridSpec(
            num_scalar_prefetch=1,
            grid=(heads_here,),
            in_specs=[own_block] * 3 + [block] * 3 + [whole, up_block, block, block],
            out_specs=(block, up_block, whole),
            scratch_shapes=[
                pltpu.VMEM((length, HDIM), jnp.bfloat16),
                pltpu.VMEM((length, HDIM), jnp.bfloat16),
                pltpu.VMEM((length, HDIM), jnp.bfloat16),
                pltpu.VMEM((HDIM, length), jnp.bfloat16),
                pltpu.VMEM((HDIM, length), jnp.bfloat16),
                pltpu.VMEM((length, HDIM), jnp.bfloat16),
                pltpu.VMEM((length, HDIM), jnp.float32),
                pltpu.VMEM((length, HDIM), jnp.float32),
                pltpu.VMEM((length, ranks), jnp.float32),
            ],
        ),
        compiler_params=pltpu.CompilerParams(
            dimension_semantics=("arbitrary",), vmem_limit_bytes=VMEM_LIMIT
        ),
        cost_estimate=pl.CostEstimate(
            flops=12 * heads_here * length * length * HDIM,
            bytes_accessed=24 * length * columns,
            transcendentals=heads_here * length * length,
        ),
        name="student",
    )(cfg_index[None], *own, *sent, rank_all, up_here, target_own, target_sent)


def exchanged(blocks, axis):
    return lax.all_to_all(blocks, axis, split_axis=0, concat_axis=0, tiled=True)


def gathered(value, axis):
    count = lax.axis_size(axis)
    return exchanged(jnp.broadcast_to(value[None], (count,) + value.shape), axis)


def body(
    teacher_query,
    teacher_key,
    teacher_value,
    hidden,
    adapter_down_weight,
    adapter_up_weight,
    guidance_index,
    timestep_index,
):
    cfg_index = lax.axis_index("cfg")
    seq_index = lax.axis_index("seq")
    seq_count = lax.axis_size("seq")
    dp_count = lax.axis_size("dp")
    tok_here = hidden.shape[2]
    length = tok_here * seq_count
    total_rows = 2 * dp_count * length
    ranks = 3 * ADAPTER_RANK
    input_features = hidden[0, 0]
    model_width = input_features.shape[1]
    half_cols = model_width // (2 * seq_count)

    guide_scale = 1.0 + 0.5 * guidance_index[:, 0].astype(jnp.float32)
    time_frac = (timestep_index[:, 0].astype(jnp.float32) + 0.5) / TSTEPS
    own_scale = lax.dynamic_index_in_dim(guide_scale, cfg_index, 0, keepdims=False)
    own_time = lax.dynamic_index_in_dim(time_frac, cfg_index, 0, keepdims=False)
    weighting = jnp.where(cfg_index == 0, guide_scale, 1.0 - guide_scale)
    rank_index = jnp.arange(1, ADAPTER_RANK + 1).astype(jnp.float32)
    feature_modulation = 1.0 + 0.5 * jnp.cos(
        math.pi * rank_index * own_time + 0.25 * rank_index * own_scale
    )
    modulation = jnp.tile(feature_modulation, 3)[None]

    teacher_heads = []
    sent = []
    for field in (teacher_query, teacher_key, teacher_value):
        heads = lax.all_to_all(field[0, :, 0], "seq", split_axis=2, concat_axis=1, tiled=True)
        teacher_heads.append(heads)
        sent.append(lax.ppermute(heads[1], "cfg", [(0, 1)]))

    rank_projected = jnp.concatenate(
        [dot_f32(input_features, adapter_down_weight[member]) for member in range(3)], axis=1
    )
    rank_projected = (rank_projected * modulation).astype(jnp.bfloat16)
    rank_all = gathered(rank_projected, "seq").reshape(length, ranks)

    split_view = input_features.reshape(tok_here, 2, seq_count, half_cols)
    split_view = split_view.transpose(2, 0, 1, 3).reshape(seq_count, tok_here, 2 * half_cols)
    column_block = exchanged(split_view, "seq").reshape(length, 2 * half_cols)

    other = 1 - cfg_index
    other_weighted = teacher_attention(
        other, lax.dynamic_index_in_dim(weighting, other, 0, keepdims=False), teacher_heads
    )
    target_sent = lax.ppermute(other_weighted, "cfg", [(0, 1), (1, 0)])
    target_own = teacher_attention(
        cfg_index, lax.dynamic_index_in_dim(weighting, cfg_index, 0, keepdims=False), teacher_heads
    )

    columns = target_own.shape[1]
    up_here = lax.dynamic_slice_in_dim(adapter_up_weight, seq_index * columns, columns, axis=2)
    student_local, up_partial, back_partial = student_step(
        cfg_index, total_rows, teacher_heads, sent, rank_all, up_here, target_own, target_sent
    )

    back_parts = exchanged(back_partial.reshape(seq_count, tok_here, ranks), "seq")
    rank_backward = jnp.sum(back_parts.astype(jnp.float32), axis=0)
    low_grad = (rank_backward * modulation).astype(jnp.bfloat16)
    student_tokens = lax.all_to_all(student_local, "seq", split_axis=0, concat_axis=1, tiled=True)
    grad_rows = gathered(low_grad, "seq").reshape(length, ranks)

    groups = 2 * dp_count
    up_rows = ADAPTER_RANK // groups
    up_parts = up_partial.reshape(3, groups, up_rows, columns).transpose(1, 0, 2, 3)
    grad_up = jnp.sum(exchanged(up_parts, ("cfg", "dp")).astype(jnp.float32), axis=0)

    column_partial = lax.dot_general(
        column_block, grad_rows, TN, preferred_element_type=jnp.float32
    ).astype(jnp.bfloat16)
    down_rows = 2 * half_cols // groups
    down_parts = exchanged(column_partial.reshape(groups, down_rows, ranks), ("cfg", "dp"))
    grad_down = jnp.sum(down_parts.astype(jnp.float32), axis=0)
    grad_down = grad_down.reshape(down_rows, 3, ADAPTER_RANK).transpose(1, 0, 2)
    return (student_tokens[None, None], grad_down, grad_up)


def solution(mesh):
    placed = (
        P("cfg", None, "dp", "seq", None),
        P("cfg", None, "dp", "seq", None),
        P("cfg", None, "dp", "seq", None),
        P("cfg", "dp", "seq", None),
        P(),
        P(),
        P(None, "dp"),
        P(None, "dp"),
    )
    return jax.shard_map(
        body,
        mesh=mesh,
        in_specs=placed,
        out_specs=(
            P("cfg", "dp", "seq", None),
            P(None, ("cfg", "seq", "dp"), None),
            P(None, ("cfg", "dp"), "seq"),
        ),
        check_vma=False,
    )
```

time: 493 us -> 305 us (0.62)
  matrix products: 86.5 us -> 7.1 us
  blocking collectives: 68.7 us -> 23 us
  Pallas kernels: 0 us -> 39.5 us
  waiting for transfers between devices: 173 us -> 141 us
  local copies, waits for them, and re-layouts: 70.6 us -> 39.5 us
  starting transfers between devices: 65.5 us -> 48.3 us
  between operations: 15.7 us -> 2.21 us
  other arithmetic: 9.88 us -> 2.84 us
    dot_general x21 -> x4, matrix products: 52.9 us -> 7.1 us  [the longest x3 4.67 us: dot_f32(): return jnp.dot(left, right, preferred_element_type=jnp.float32)]
    pallas_call x0 -> x3, Pallas kernels: none -> 39.5 us  [the longest x1 21 us: student_step(): pl.pallas_call(functools.partial(student_kernel, step_rows, 1.0 / math.sq...]
    sub x8 -> x0, matrix products: 33.6 us -> none  [head_probs(): raised = jnp.exp(scores - highest)]
    all_gather x1 -> x0, blocking collectives: 32.7 us -> none  [body(): grad_rows = lax.all_gather(low_grad, 'seq', axis=1, tiled=True)]
    ppermute x3 -> x4, waiting for transfers between devices: 0.01 us -> 22 us  [the longest x3 22 us: body(): sent.append(lax.ppermute(heads[1], 'cfg', [(0, 1)]))]
    reduce_scatter x3 -> x0, waiting for transfers between devices: 21.4 us -> none  [the longest x1 20.3 us: body(): lax.psum_scatter(per_seq, ('cfg', 'dp'), scatter_dimension=1, tiled=True)]
    unnamed x5 -> x0, waiting for transfers between devices: 18.4 us -> none
    all_to_all x11 -> x8, starting transfers between devices: 51.3 us -> 35.8 us  [the longest x5 20 us: exchanged(): return lax.all_to_all(blocks, axis, split_axis=0, concat_axis=0, tiled=True)]
  transfers between devices with their start and end apart: 19 -> 13, of which waited for: 13 -> 11; matrix products, arithmetic and copies ran while one was open for 23% -> 12% of each run, Pallas kernels for 0% -> 6%
where the time goes in v1:
time: 305 us; the launch traced here: 303 us
  waiting for transfers between devices  141 us (46%)
  starting transfers between devices  48.3 us (16%)
  local copies, waits for them, and re-layouts  39.5 us (13%)
  Pallas kernels  39.5 us (13%)
  blocking collectives  23 us (8%)
  matrix products  7.1 us (2%)
    all_to_all x3, waiting for transfers between devices, body(): lax.all_to_all(field[0, :, 0], 'seq', split_axis=2, concat_axis=1, tiled=...  62.4 us
    all_to_all x5, waiting for transfers between devices, exchanged(): return lax.all_to_all(blocks, axis, split_axis=0, concat_axis=0, tiled=True)  44.8 us
    all_to_all x1, blocking collectives, exchanged(): return lax.all_to_all(blocks, axis, split_axis=0, concat_axis=0, tiled=True)  23 us
    ppermute x3, waiting for transfers between devices, body(): sent.append(lax.ppermute(heads[1], 'cfg', [(0, 1)]))  22 us
    unnamed x35, local copies, waits for them, and re-layouts  21.2 us
    pallas_call x1, Pallas kernels, student_step(): pl.pallas_call(functools.partial(student_kernel, step_rows, 1.0 / math.sq...  21 us
    all_to_all x5, starting transfers between devices, exchanged(): return lax.all_to_all(blocks, axis, split_axis=0, concat_axis=0, tiled=True)  20 us
    pallas_call x2, Pallas kernels, teacher_attention(): pl.pallas_call(functools.partial(teacher_kernel, step_rows), out_shape=ja...  18.5 us
  transfers between devices with their start and end apart: 13, of which 11 were waited for; matrix products, arithmetic and copies ran while one was open for 12% of the time, Pallas kernels for 6%

profile of v1, /device:TPU:0, one launch (start us, length us, event | category | flops | bytes accessed | tf_op | source)
XLA Modules:
  0.0 303.4 jit_solution(38230707244301930)
XLA Ops:
  0.6 3.8 %copy.31 = bf16[1,2,1,128,2048]{3,1,4,2,0:T(2,128)(2,1)} copy(bf16[1,2,1,128,2048]{4,3,2,1,0:T(8,128)(2,1)} %param.10) | data formatting | bytes 2097152 | tf_op args[2]
  4.4 7.3 %all-to-all-start.2 = ((bf16[2,128,2048]{1,0,2:T(2,128)(2,1)}), bf16[2,128,2048]{1,0,2:T(2,128)(2,1)S(1)}, u32[]{:S(2)}, u32[]{:S(2)}) async-start(bf16[2,128,2048]{1,0,2:T(2,128)(2,1)} %bitcast.80), calls=%async_computation.2 | async-start | bytes 2097152 | tf_op jit(solution)/shard_map/all_to_all | solution.py:255
  11.8 3.7 %copy.27 = bf16[1,2,1,128,2048]{3,1,4,2,0:T(2,128)(2,1)} copy(bf16[1,2,1,128,2048]{4,3,2,1,0:T(8,128)(2,1)} %param.8) | data formatting | bytes 2097152 | tf_op args[0]
  15.4 22.1 %all-to-all-done.2 = bf16[2,128,2048]{1,0,2:T(2,128)(2,1)S(1)} async-done(((bf16[2,128,2048]{1,0,2:T(2,128)(2,1)}), bf16[2,128,2048]{1,0,2:T(2,128)(2,1)S(1)}, u32[]{:S(2)}, u32[]{:S(2)}) %all-to-all-start.2) | async-done | bytes 1048608 | tf_op jit(solution)/shard_map/all_to_all | solution.py:255
  37.5 4.2 %all-to-all-start = ((bf16[2,128,2048]{1,0,2:T(2,128)(2,1)}), bf16[2,128,2048]{1,0,2:T(2,128)(2,1)}, u32[]{:S(2)}, u32[]{:S(2)}) async-start(bf16[2,128,2048]{1,0,2:T(2,128)(2,1)} %bitcast.79), calls=%async_computation | async-start | bytes 2097152 | tf_op jit(solution)/shard_map/all_to_all | solution.py:255
  41.8 3.8 %copy.29 = bf16[1,2,1,128,2048]{3,1,4,2,0:T(2,128)(2,1)} copy(bf16[1,2,1,128,2048]{4,3,2,1,0:T(8,128)(2,1)} %param.9) | data formatting | bytes 2097152 | tf_op args[1]
  45.6 21.8 %all-to-all-done = bf16[2,128,2048]{1,0,2:T(2,128)(2,1)} async-done(((bf16[2,128,2048]{1,0,2:T(2,128)(2,1)}), bf16[2,128,2048]{1,0,2:T(2,128)(2,1)}, u32[]{:S(2)}, u32[]{:S(2)}) %all-to-all-start) | async-done | bytes 1048608 | tf_op jit(solution)/shard_map/all_to_all | solution.py:255
  67.3 4.2 %all-to-all-start.1 = ((bf16[2,128,2048]{1,0,2:T(2,128)(2,1)}), bf16[2,128,2048]{1,0,2:T(2,128)(2,1)}, u32[]{:S(2)}, u32[]{:S(2)}) async-start(bf16[2,128,2048]{1,0,2:T(2,128)(2,1)} %bitcast.78), calls=%async_computation.1 | async-start | bytes 2097152 | tf_op jit(solution)/shard_map/all_to_all | solution.py:255
  71.6 0.6 fusion.17
  73.6 1.6 fusion.1
  75.2 1.6 fusion.3
  76.7 1.6 fusion.5
  78.4 0.1 copy.33
  78.5 18.5 %all-to-all-done.1 = bf16[2,128,2048]{1,0,2:T(2,128)(2,1)} async-done(((bf16[2,128,2048]{1,0,2:T(2,128)(2,1)}), bf16[2,128,2048]{1,0,2:T(2,128)(2,1)}, u32[]{:S(2)}, u32[]{:S(2)}) %all-to-all-start.1) | async-done | bytes 1048608 | tf_op jit(solution)/shard_map/all_to_all | solution.py:255
  97.0 1.0 broadcast_in_dim.11
  98.0 3.5 %all-to-all-start.3 = ((bf16[8,128,384]{2,1,0:T(8,128)(2,1)}), bf16[8,128,384]{2,1,0:T(8,128)(2,1)S(1)}, u32[]{:S(2)}, u32[]{:S(2)}) async-start(bf16[8,128,384]{2,1,0:T(8,128)(2,1)} %broadcast_in_dim.11), calls=%async_computation.3 | async-start | bytes 1572864 | tf_op jit(solution)/shard_map/all_to_all | solution.py:211
  101.6 0.7 fusion.16
  102.2 2.4 copy.32
  104.7 3.8 %copy.28 = bf16[2,128,8,256]{3,1,2,0:T(8,128)(2,1)} copy(bf16[2,128,8,256]{1,0,3,2:T(2,128)(2,1)} %bitcast.2) | data formatting | bytes 2097152 | tf_op jit(solution)/shard_map/all_to_all | solution.py:255
  108.5 3.7 %copy.30 = bf16[2,128,8,256]{3,1,2,0:T(8,128)(2,1)} copy(bf16[2,128,8,256]{1,0,3,2:T(2,128)(2,1)} %bitcast.6) | data formatting | bytes 2097152 | tf_op jit(solution)/shard_map/all_to_all | solution.py:255
  112.2 1.2 copy-done.2
  113.4 1.2 copy-done.5
  114.7 9.5 %teacher.3 = bf16[1024,256]{1,0:T(8,128)(2,1)} custom-call(s32[1]{0:T(128)} %bitcast.27.half_ref, f32[1]{0:T(128)} %get-tuple-element.15.weight_ref, bf16[2,1024,256]{2,1,0:T(8,128)(2,1)S(1)} %bitcast.67, bf16[2,1024,256]{2,1,0:T(8,128)(2,1)S(1)} %bitcast.72, bf16[2,1024,256]{2,1,0:T(8,128)(2,1)S(1)} %bitcast.63), custom_call_target="tpu_custom_call" | custom-call | flops 1073741824 | bytes 2097152 | tf_op jit(solution)/shard_map/teacher/pallas_call | solution.py:57
  124.2 1.5 collective-permute-start.3
  125.7 0.8 slice.27
  126.5 3.2 %collective-permute-start = (bf16[1024,256]{1,0:T(8,128)(2,1)}, bf16[1024,256]{1,0:T(8,128)(2,1)}, u32[]{:S(2)}, u32[]{:S(2)}) collective-permute-start(bf16[1024,256]{1,0:T(8,128)(2,1)} %bitcast.13), channel_id=1, source_target_pairs={{0,16},{1,17},{2,18},{3,19},{4,20},{5,21},{6,22},{7,23},{8,24},{9,... | collective-permute-start | bytes 1572872 | tf_op jit(solution)/shard_map/ppermute | solution.py:257
  129.8 0.8 slice.28
  130.6 2.1 collective-permute-start.1
  132.7 0.8 slice.29
  133.5 2.1 collective-permute-start.2
  135.6 0.7 constant_dynamic-slice_fusion.up_ref
  136.3 1.2 copy-done.3
  137.6 1.2 copy-done.6
  138.8 9.0 %teacher.2.target_own = bf16[1024,256]{1,0:T(8,128)(2,1)S(1)} custom-call(s32[1]{0:T(128)} %bitcast.half_ref.cfg_ref, f32[1]{0:T(128)} %get-tuple-element.16.weight_ref, bf16[2,1024,256]{2,1,0:T(8,128)(2,1)S(1)} %bitcast.69, bf16[2,1024,256]{2,1,0:T(8,128)(2,1)S(1)} %bitcast.74, bf16[2,1024,256]{2,1,0:T(8,128)(2,1)S(1)} %bitcast.65), custom_call_target="tpu_custom_call" | custom-call | flops 1073741824 | bytes 2097152 | tf_op jit(solution)/shard_map/teacher/pallas_call | solution.py:57
  147.8 0.8 copy-done.8
  148.6 1.0 collective-permute-done.sent_query
  149.6 11.2 %collective-permute-done.1.sent_key = bf16[1024,256]{1,0:T(8,128)(2,1)} collective-permute-done((bf16[1024,256]{1,0:T(8,128)(2,1)}, bf16[1024,256]{1,0:T(8,128)(2,1)}, u32[]{:S(2)}, u32[]{:S(2)}) %collective-permute-start.1) | collective-permute-done | bytes 524320 | tf_op jit(solution)/shard_map/ppermute | solution.py:257
  160.8 9.8 %collective-permute-done.2.sent_value = bf16[1024,256]{1,0:T(8,128)(2,1)} collective-permute-done((bf16[1024,256]{1,0:T(8,128)(2,1)}, bf16[1024,256]{1,0:T(8,128)(2,1)}, u32[]{:S(2)}, u32[]{:S(2)}) %collective-permute-start.2) | collective-permute-done | bytes 524320 | tf_op jit(solution)/shard_map/ppermute | solution.py:257
  170.6 1.2 copy-done.4
  171.8 0.9 copy-done.7
  172.8 1.0 copy-done.9
  173.8 21.0 %student.1 = (bf16[1024,256]{1,0:T(8,128)(2,1)}, bf16[3,128,256]{2,1,0:T(8,128)(2,1)S(1)}, bf16[1024,384]{1,0:T(8,128)(2,1)}) custom-call(s32[1]{0:T(128)} %bitcast.half_ref.cfg_ref, bf16[2,1024,256]{2,1,0:T(8,128)(2,1)S(1)} %bitcast.70, bf16[2,1024,256]{2,1,0:T(8,128)(2,1)} %bitcast.71, bf16[2,1024,256]{2,1,0:T(8,128)(2,1)} %bitcast.66, ...), custom_call_target="tpu_custom_call" | custom-call | flops 3221225472 | bytes 6291456 | tf_op jit(solution)/shard_map/student/pallas_call | solution.py:174
  194.8 5.7 %all-to-all-start.5 = ((bf16[8,128,384]{2,1,0:T(8,128)(2,1)}), bf16[8,128,384]{2,1,0:T(8,128)(2,1)}, u32[]{:S(2)}, u32[]{:S(2)}) async-start(bf16[8,128,384]{2,1,0:T(8,128)(2,1)} %bitcast.30), calls=%async_computation.5 | async-start | bytes 1572864 | tf_op jit(solution)/shard_map/all_to_all | solution.py:211
  200.5 0.4 copy.37
  200.9 1.0 copy.38
  201.9 17.6 %all-to-all-done.5 = bf16[8,128,384]{2,1,0:T(8,128)(2,1)} async-done(((bf16[8,128,384]{2,1,0:T(8,128)(2,1)}), bf16[8,128,384]{2,1,0:T(8,128)(2,1)}, u32[]{:S(2)}, u32[]{:S(2)}) %all-to-all-start.5) | async-done | bytes 786464 | tf_op jit(solution)/shard_map/all_to_all | solution.py:211
  219.5 3.5 %all-to-all-start.7 = ((bf16[8,128,384]{1,2,0:T(8,128)(2,1)}), bf16[8,128,384]{1,2,0:T(8,128)(2,1)S(1)}, u32[]{:S(2)}, u32[]{:S(2)}) async-start(bf16[8,128,384]{1,2,0:T(8,128)(2,1)} %bitcast.33), calls=%async_computation.7 | async-start | bytes 1572864 | tf_op jit(solution)/shard_map/all_to_all | solution.py:211
  223.1 0.7 copy.42
  223.8 1.3 convert_reduce_fusion
  225.0 0.1 copy.35
  225.2 17.8 %all-to-all-done.7 = bf16[8,128,384]{1,2,0:T(8,128)(2,1)S(1)} async-done(((bf16[8,128,384]{1,2,0:T(8,128)(2,1)}), bf16[8,128,384]{1,2,0:T(8,128)(2,1)S(1)}, u32[]{:S(2)}, u32[]{:S(2)}) %all-to-all-start.7) | async-done | bytes 786464 | tf_op jit(solution)/shard_map/all_to_all | solution.py:211
  243.0 3.8 %all-to-all-start.9 = ((bf16[4,3,32,256]{3,2,1,0:T(8,128)(2,1)}), bf16[4,3,32,256]{3,2,1,0:T(8,128)(2,1)S(1)}, u32[]{:S(2)}, u32[]{:S(2)}) async-start(bf16[4,3,32,256]{3,2,1,0:T(8,128)(2,1)} %bitcast.62), calls=%async_computation.9 | async-start | bytes 393216 | tf_op jit(solution)/shard_map/all_to_all | solution.py:211
  246.9 0.1 copy.36
  247.0 5.1 %all-to-all-done.9 = bf16[4,3,32,256]{3,2,1,0:T(8,128)(2,1)S(1)} async-done(((bf16[4,3,32,256]{3,2,1,0:T(8,128)(2,1)}), bf16[4,3,32,256]{3,2,1,0:T(8,128)(2,1)S(1)}, u32[]{:S(2)}, u32[]{:S(2)}) %all-to-all-start.9) | async-done | bytes 196640 | tf_op jit(solution)/shard_map/all_to_all | solution.py:211
  252.1 23.0 %all_to_all.100 = bf16[8,128,384]{2,1,0:T(8,128)(2,1)} all-to-all(bf16[8,128,384]{2,1,0:T(8,128)(2,1)S(1)} %broadcast_in_dim.28), channel_id=1, replica_groups=mesh['cfg'=2,'seq'=8,'dp'=2] {'seq'}, dimensions={0} | all-to-all | bytes 1572864 | tf_op jit(solution)/shard_map/all_to_all | solution.py:211
  275.1 3.6 %all-to-all-start.4 = ((bf16[8,128,256]{2,1,0:T(8,128)(2,1)}), bf16[8,128,256]{2,1,0:T(8,128)(2,1)S(1)}, u32[]{:S(2)}, u32[]{:S(2)}) async-start(bf16[8,128,256]{2,1,0:T(8,128)(2,1)} %bitcast.28), calls=%async_computation.4 | async-start | bytes 1048576 | tf_op jit(solution)/shard_map/all_to_all | solution.py:287
  278.7 2.4 fusion
  281.1 11.7 %all-to-all-done.4 = bf16[8,128,256]{2,1,0:T(8,128)(2,1)S(1)} async-done(((bf16[8,128,256]{2,1,0:T(8,128)(2,1)}), bf16[8,128,256]{2,1,0:T(8,128)(2,1)S(1)}, u32[]{:S(2)}, u32[]{:S(2)}) %all-to-all-start.4) | async-done | bytes 524320 | tf_op jit(solution)/shard_map/all_to_all | solution.py:287
  292.8 3.5 %all-to-all-start.8 = ((bf16[4,96,384]{2,1,0:T(8,128)(2,1)}), bf16[4,96,384]{2,1,0:T(8,128)(2,1)S(1)}, u32[]{:S(2)}, u32[]{:S(2)}) async-start(bf16[4,96,384]{2,1,0:T(8,128)(2,1)} %bitcast.84), calls=%async_computation.8 | async-start | bytes 589824 | tf_op jit(solution)/shard_map/all_to_all | solution.py:211
  296.3 0.7 convert_reduce_fusion.2
  296.9 0.3 copy.34
  297.2 1.0 broadcast_in_dim.13
  298.3 4.3 %all-to-all-done.8 = bf16[4,96,384]{2,1,0:T(8,128)(2,1)S(1)} async-done(((bf16[4,96,384]{2,1,0:T(8,128)(2,1)}), bf16[4,96,384]{2,1,0:T(8,128)(2,1)S(1)}, u32[]{:S(2)}, u32[]{:S(2)}) %all-to-all-start.8) | async-done | bytes 294944 | tf_op jit(solution)/shard_map/all_to_all | solution.py:211
  302.7 0.7 copy.40
  (34 shorter events, 0.5 us)
Async XLA Ops:
  0.6 135.0 %copy-start = (bf16[3,128,2048]{2,1,0:T(8,128)(2,1)S(1)}, bf16[3,128,2048]{2,1,0:T(8,128)(2,1)}, u32[]{:S(2)}) copy-start(bf16[3,128,2048]{2,1,0:T(8,128)(2,1)} %param.13) | copy-start | bytes 4718596
  4.4 33.1 %all-to-all-start.2 = ((bf16[2,128,2048]{1,0,2:T(2,128)(2,1)}), bf16[2,128,2048]{1,0,2:T(2,128)(2,1)S(1)}, u32[]{:S(2)}, u32[]{:S(2)}) async-start(bf16[2,128,2048]{1,0,2:T(2,128)(2,1)} %bitcast.80), calls=%async_computation.2 | async-start | bytes 2097152 | tf_op jit(solution)/shard_map/all_to_all | solution.py:255
  37.5 29.8 %copy-start.12 = (bf16[2,128,2048]{1,0,2:T(2,128)(2,1)}, bf16[2,128,2048]{1,0,2:T(2,128)(2,1)S(1)}, u32[]{:S(2)}) copy-start(bf16[2,128,2048]{1,0,2:T(2,128)(2,1)S(1)} %all-to-all-done.2) | copy-start | bytes 3145732
  37.5 29.8 %all-to-all-start = ((bf16[2,128,2048]{1,0,2:T(2,128)(2,1)}), bf16[2,128,2048]{1,0,2:T(2,128)(2,1)}, u32[]{:S(2)}, u32[]{:S(2)}) async-start(bf16[2,128,2048]{1,0,2:T(2,128)(2,1)} %bitcast.79), calls=%async_computation | async-start | bytes 2097152 | tf_op jit(solution)/shard_map/all_to_all | solution.py:255
  41.8 29.8 %copy-start.13 = (s32[2,1]{0,1:T(1,128)S(1)}, s32[2,1]{0,1:T(1,128)}, u32[]{:S(2)}) copy-start(s32[2,1]{0,1:T(1,128)} %param.15) | copy-start | bytes 28
  41.8 29.8 %copy-start.14 = (s32[2,1]{0,1:T(1,128)S(1)}, s32[2,1]{0,1:T(1,128)}, u32[]{:S(2)}) copy-start(s32[2,1]{0,1:T(1,128)} %param.14) | copy-start | bytes 28
  41.8 31.8 %copy-start.10 = (bf16[1,1,128,3072]{3,2,1,0:T(8,128)(2,1)S(1)}, bf16[1,1,128,3072]{3,2,1,0:T(8,128)(2,1)}, u32[]{:S(2)}) copy-start(bf16[1,1,128,3072]{3,2,1,0:T(8,128)(2,1)} %param.11) | copy-start | bytes 2359300
  67.3 29.7 %all-to-all-start.1 = ((bf16[2,128,2048]{1,0,2:T(2,128)(2,1)}), bf16[2,128,2048]{1,0,2:T(2,128)(2,1)}, u32[]{:S(2)}, u32[]{:S(2)}) async-start(bf16[2,128,2048]{1,0,2:T(2,128)(2,1)} %bitcast.78), calls=%async_computation.1 | async-start | bytes 2097152 | tf_op jit(solution)/shard_map/all_to_all | solution.py:255
  98.0 50.6 %all-to-all-start.3 = ((bf16[8,128,384]{2,1,0:T(8,128)(2,1)}), bf16[8,128,384]{2,1,0:T(8,128)(2,1)S(1)}, u32[]{:S(2)}, u32[]{:S(2)}) async-start(bf16[8,128,384]{2,1,0:T(8,128)(2,1)} %broadcast_in_dim.11), calls=%async_computation.3 | async-start | bytes 1572864 | tf_op jit(solution)/shard_map/all_to_all | solution.py:211
  104.7 31.7 %copy-start.1 = (bf16[2,128,8,256]{3,1,2,0:T(8,128)(2,1)}, bf16[2,128,8,256]{3,1,2,0:T(8,128)(2,1)S(1)}, u32[]{:S(2)}) copy-start(bf16[2,128,8,256]{3,1,2,0:T(8,128)(2,1)S(1)} %copy.32) | copy-start | bytes 3145732
  112.2 1.2 copy-start.2
  113.4 1.2 copy-start.5
  124.2 24.4 %collective-permute-start.3 = (bf16[1024,256]{1,0:T(8,128)(2,1)}, bf16[1024,256]{1,0:T(8,128)(2,1)}, u32[]{:S(2)}, u32[]{:S(2)}) collective-permute-start(bf16[1024,256]{1,0:T(8,128)(2,1)} %teacher.3), channel_id=1, source_target_pairs={{0,16},{16,0},{1,17},{17,1},{2,18},{18,2},{3,19},{19,3},{4,20},{20... | collective-permute-start | bytes 1572872 | tf_op jit(solution)/shard_map/ppermute | solution.py:273
  126.5 23.0 %collective-permute-start = (bf16[1024,256]{1,0:T(8,128)(2,1)}, bf16[1024,256]{1,0:T(8,128)(2,1)}, u32[]{:S(2)}, u32[]{:S(2)}) collective-permute-start(bf16[1024,256]{1,0:T(8,128)(2,1)} %bitcast.13), channel_id=1, source_target_pairs={{0,16},{1,17},{2,18},{3,19},{4,20},{5,21},{6,22},{7,23},{8,24},{9,... | collective-permute-start | bytes 1572872 | tf_op jit(solution)/shard_map/ppermute | solution.py:257
  130.6 30.2 %collective-permute-start.1 = (bf16[1024,256]{1,0:T(8,128)(2,1)}, bf16[1024,256]{1,0:T(8,128)(2,1)}, u32[]{:S(2)}, u32[]{:S(2)}) collective-permute-start(bf16[1024,256]{1,0:T(8,128)(2,1)} %bitcast.14), channel_id=1, source_target_pairs={{0,16},{1,17},{2,18},{3,19},{4,20},{5,21},{6,22},{7,23},{8,24},{9,... | collective-permute-start | bytes 1572872 | tf_op jit(solution)/shard_map/ppermute | solution.py:257
  133.5 37.1 %collective-permute-start.2 = (bf16[1024,256]{1,0:T(8,128)(2,1)}, bf16[1024,256]{1,0:T(8,128)(2,1)}, u32[]{:S(2)}, u32[]{:S(2)}) collective-permute-start(bf16[1024,256]{1,0:T(8,128)(2,1)} %bitcast.15), channel_id=1, source_target_pairs={{0,16},{1,17},{2,18},{3,19},{4,20},{5,21},{6,22},{7,23},{8,24},{9,... | collective-permute-start | bytes 1572872 | tf_op jit(solution)/shard_map/ppermute | solution.py:257
  136.3 1.2 copy-start.3
  137.6 1.2 copy-start.6
  147.8 0.8 copy-start.8
  170.6 1.2 copy-start.4
  171.8 0.9 copy-start.7
  172.8 1.0 copy-start.9
  173.8 26.7 %copy-start.11 = (bf16[1,1,128,3072]{3,2,1,0:T(8,128)(2,1)S(1)}, bf16[1,1,128,3072]{3,2,1,0:T(8,128)(2,1)}, u32[]{:S(2)}) copy-start(bf16[1,1,128,3072]{3,2,1,0:T(8,128)(2,1)} %param.11) | copy-start | bytes 2359300
  194.8 24.7 %all-to-all-start.5 = ((bf16[8,128,384]{2,1,0:T(8,128)(2,1)}), bf16[8,128,384]{2,1,0:T(8,128)(2,1)}, u32[]{:S(2)}, u32[]{:S(2)}) async-start(bf16[8,128,384]{2,1,0:T(8,128)(2,1)} %bitcast.30), calls=%async_computation.5 | async-start | bytes 1572864 | tf_op jit(solution)/shard_map/all_to_all | solution.py:211
  219.5 23.5 %all-to-all-start.7 = ((bf16[8,128,384]{1,2,0:T(8,128)(2,1)}), bf16[8,128,384]{1,2,0:T(8,128)(2,1)S(1)}, u32[]{:S(2)}, u32[]{:S(2)}) async-start(bf16[8,128,384]{1,2,0:T(8,128)(2,1)} %bitcast.33), calls=%async_computation.7 | async-start | bytes 1572864 | tf_op jit(solution)/shard_map/all_to_all | solution.py:211
  243.0 9.1 %all-to-all-start.9 = ((bf16[4,3,32,256]{3,2,1,0:T(8,128)(2,1)}), bf16[4,3,32,256]{3,2,1,0:T(8,128)(2,1)S(1)}, u32[]{:S(2)}, u32[]{:S(2)}) async-start(bf16[4,3,32,256]{3,2,1,0:T(8,128)(2,1)} %bitcast.62), calls=%async_computation.9 | async-start | bytes 393216 | tf_op jit(solution)/shard_map/all_to_all | solution.py:211
  275.1 17.7 %all-to-all-start.4 = ((bf16[8,128,256]{2,1,0:T(8,128)(2,1)}), bf16[8,128,256]{2,1,0:T(8,128)(2,1)S(1)}, u32[]{:S(2)}, u32[]{:S(2)}) async-start(bf16[8,128,256]{2,1,0:T(8,128)(2,1)} %bitcast.28), calls=%async_computation.4 | async-start | bytes 1048576 | tf_op jit(solution)/shard_map/all_to_all | solution.py:287
  292.8 9.8 %all-to-all-start.8 = ((bf16[4,96,384]{2,1,0:T(8,128)(2,1)}), bf16[4,96,384]{2,1,0:T(8,128)(2,1)S(1)}, u32[]{:S(2)}, u32[]{:S(2)}) async-start(bf16[4,96,384]{2,1,0:T(8,128)(2,1)} %bitcast.84), calls=%async_computation.8 | async-start | bytes 589824 | tf_op jit(solution)/shard_map/all_to_all | solution.py:211

commit v2 on v1

--- a/solution.py
+++ b/solution.py
@@ -7,6 +7,7 @@
 from jax.experimental import pallas as pl
 from jax.experimental.pallas import tpu as pltpu
 from jax.sharding import PartitionSpec as P
+
 
 HDIM = 128
 ADAPTER_RANK = 128
@@ -207,6 +208,130 @@
     )(cfg_index[None], *own, *sent, rank_all, up_here, target_own, target_sent)
 
 
+def scatter_kernel(count, *refs):
+    fields = refs[0:3]
+    heads = refs[3:6]
+    sent = refs[6:9]
+    kept, send_sem, recv_sem, pass_send_sem, pass_recv_sem, load_sem, store_sem = refs[9:]
+    me = lax.axis_index("seq")
+    cfg_index = lax.axis_index("cfg")
+    tok_here = fields[0].shape[1]
+    columns = heads[0].shape[2]
+
+    loads = []
+    own_columns = pl.ds(pl.multiple_of(me * columns, columns), columns)
+    own_rows = pl.ds(pl.multiple_of(me * tok_here, tok_here), tok_here)
+    for member in range(3):
+        load = pltpu.make_async_copy(
+            fields[member].at[:, :, own_columns], kept.at[member], load_sem.at[member]
+        )
+        load.start()
+        loads.append(load)
+
+    barrier = pltpu.get_barrier_semaphore()
+    for step in range(1, count):
+        pl.semaphore_signal(
+            barrier,
+            inc=1,
+            device_id={"seq": lax.rem(me + step, count)},
+            device_id_type=pl.DeviceIdType.MESH,
+        )
+    pl.semaphore_signal(
+        barrier, inc=1, device_id={"cfg": 1 - cfg_index}, device_id_type=pl.DeviceIdType.MESH
+    )
+    pl.semaphore_wait(barrier, count)
+
+    def scattered(member, step):
+        peer = lax.rem(me + step, count)
+        peer_columns = pl.ds(pl.multiple_of(peer * columns, columns), columns)
+        return pltpu.make_async_remote_copy(
+            src_ref=fields[member].at[:, :, peer_columns],
+            dst_ref=heads[member].at[:, own_rows, :],
+            send_sem=send_sem.at[member, step],
+            recv_sem=recv_sem.at[member, step],
+            device_id={"seq": peer},
+            device_id_type=pl.DeviceIdType.MESH,
+        )
+
+    def passed(member, step):
+        source = lax.rem(me - step + count, count)
+        rows = pl.ds(pl.multiple_of(source * tok_here, tok_here), tok_here)
+        block = kept.at[member, 1] if step == 0 else heads[member].at[1, rows, :]
+        return pltpu.make_async_remote_copy(
+            src_ref=block,
+            dst_ref=sent[member].at[rows, :],
+            send_sem=pass_send_sem.at[member, step],
+            recv_sem=pass_recv_sem.at[member, step],
+            device_id={"cfg": 1 - cfg_index},
+            device_id_type=pl.DeviceIdType.MESH,
+        )
+
+    for member in range(3):
+        for step in range(1, count):
+            scattered(member, step).start()
+
+    stores = []
+    for member in range(3):
+        loads[member].wait()
+        store = pltpu.make_async_copy(
+            kept.at[member], heads[member].at[:, own_rows, :], store_sem.at[member]
+        )
+        store.start()
+        stores.append(store)
+
+    for member in range(3):
+        for step in range(count):
+            if step > 0:
+                scattered(member, step).wait_recv()
+
+            @pl.when(cfg_index == 0)
+            def _():
+                passed(member, step).start()
+
+    for member in range(3):
+        stores[member].wait()
+        for step in range(count):
+            if step > 0:
+                scattered(member, step).wait_send()
+
+            @pl.when(cfg_index == 0)
+            def _():
+                passed(member, step).wait_send()
+
+            @pl.when(cfg_index == 1)
+            def _():
+                passed(member, step).wait_recv()
+
+
+def scatter_teacher(fields):
+    count = lax.axis_size("seq")
+    halves, tok_here, width = fields[0].shape
+    length, columns = tok_here * count, width // count
+    any_spec = pl.BlockSpec(memory_space=pl.ANY)
+    outs = pl.pallas_call(
+        functools.partial(scatter_kernel, count),
+        out_shape=[jax.ShapeDtypeStruct((halves, length, columns), jnp.bfloat16)] * 3
+        + [jax.ShapeDtypeStruct((length, columns), jnp.bfloat16)] * 3,
+        in_specs=[any_spec] * 3,
+        out_specs=[any_spec] * 6,
+        scratch_shapes=[
+            pltpu.VMEM((3, halves, tok_here, columns), jnp.bfloat16),
+            pltpu.SemaphoreType.DMA((3, count)),
+            pltpu.SemaphoreType.DMA((3, count)),
+            pltpu.SemaphoreType.DMA((3, count)),
+            pltpu.SemaphoreType.DMA((3, count)),
+            pltpu.SemaphoreType.DMA((3,)),
+            pltpu.SemaphoreType.DMA((3,)),
+        ],
+        compiler_params=pltpu.CompilerParams(collective_id=0, has_side_effects=True),
+        cost_estimate=pl.CostEstimate(
+            flops=0, bytes_accessed=12 * halves * length * columns, transcendentals=0
+        ),
+        name="scatter",
+    )(*fields)
+    return outs[0:3], outs[3:6]
+
+
 def exchanged(blocks, axis):
     return lax.all_to_all(blocks, axis, split_axis=0, concat_axis=0, tiled=True)
 
@@ -249,22 +374,23 @@
     )
     modulation = jnp.tile(feature_modulation, 3)[None]
 
-    teacher_heads = []
-    sent = []
-    for field in (teacher_query, teacher_key, teacher_value):
-        heads = lax.all_to_all(field[0, :, 0], "seq", split_axis=2, concat_axis=1, tiled=True)
-        teacher_heads.append(heads)
-        sent.append(lax.ppermute(heads[1], "cfg", [(0, 1)]))
+    teacher_heads, sent = scatter_teacher(
+        (teacher_query[0, :, 0], teacher_key[0, :, 0], teacher_value[0, :, 0])
+    )
 
     rank_projected = jnp.concatenate(
         [dot_f32(input_features, adapter_down_weight[member]) for member in range(3)], axis=1
     )
     rank_projected = (rank_projected * modulation).astype(jnp.bfloat16)
-    rank_all = gathered(rank_projected, "seq").reshape(length, ranks)
+    rank_projected, *teacher_heads = lax.optimization_barrier((rank_projected, *teacher_heads))
+    rank_all = gathered(rank_projected, "seq")
+    rank_all = rank_all.reshape(length, ranks)
 
     split_view = input_features.reshape(tok_here, 2, seq_count, half_cols)
+    split_view, rank_all = lax.optimization_barrier((split_view, rank_all))
     split_view = split_view.transpose(2, 0, 1, 3).reshape(seq_count, tok_here, 2 * half_cols)
-    column_block = exchanged(split_view, "seq").reshape(length, 2 * half_cols)
+    column_block = exchanged(split_view, "seq")
+    column_block = column_block.reshape(length, 2 * half_cols)
 
     other = 1 - cfg_index
     other_weighted = teacher_attention(
@@ -272,7 +398,9 @@
     )
     target_sent = lax.ppermute(other_weighted, "cfg", [(0, 1), (1, 0)])
     target_own = teacher_attention(
-        cfg_index, lax.dynamic_index_in_dim(weighting, cfg_index, 0, keepdims=False), teacher_heads
+        cfg_index,
+        lax.dynamic_index_in_dim(weighting, cfg_index, 0, keepdims=False),
+        teacher_heads,
     )
 
     columns = target_own.shape[1]
@@ -281,6 +409,9 @@
         cfg_index, total_rows, teacher_heads, sent, rank_all, up_here, target_own, target_sent
     )
 
+    student_local, up_partial, back_partial, column_block = lax.optimization_barrier(
+        (student_local, up_partial, back_partial, column_block)
+    )
     back_parts = exchanged(back_partial.reshape(seq_count, tok_here, ranks), "seq")
     rank_backward = jnp.sum(back_parts.astype(jnp.float32), axis=0)
     low_grad = (rank_backward * modulation).astype(jnp.bfloat16)

time: 305 us -> 254 us (0.83)
  waiting for transfers between devices: 141 us -> 53.7 us
  Pallas kernels: 39.5 us -> 114 us
  local copies, waits for them, and re-layouts: 39.5 us -> 16.7 us
  starting transfers between devices: 48.3 us -> 33.4 us
    pallas_call x0 -> x1, Pallas kernels: none -> 74.4 us  [scatter_teacher(): pl.pallas_call(functools.partial(scatter_kernel, count), out_shape=[jax.S...]
    all_to_all x3 -> x0, waiting for transfers between devices: 62.4 us -> none  [body(): lax.all_to_all(field[0, :, 0], 'seq', split_axis=2, concat_axis=1, tiled=...]
    ppermute x3 -> x0, waiting for transfers between devices: 22 us -> none  [body(): sent.append(lax.ppermute(heads[1], 'cfg', [(0, 1)]))]
    all_to_all x3 -> x0, starting transfers between devices: 15.8 us -> none  [body(): lax.all_to_all(field[0, :, 0], 'seq', split_axis=2, concat_axis=1, tiled=...]
    unnamed x35 -> x28, local copies, waits for them, and re-layouts: 21.2 us -> 8.08 us
    all_to_all x3 -> x1, local copies, waits for them, and re-layouts: 9.95 us -> 1.48 us  [exchanged(): return lax.all_to_all(blocks, axis, split_axis=0, concat_axis=0, tiled=True)]
    ppermute x3 -> x0, starting transfers between devices: 7.43 us -> none  [body(): sent.append(lax.ppermute(heads[1], 'cfg', [(0, 1)]))]
    all_to_all x5, starting transfers between devices: 20 us -> 27.4 us  [exchanged(): return lax.all_to_all(blocks, axis, split_axis=0, concat_axis=0, tiled=True)]
  transfers between devices with their start and end apart: 13 -> 7, of which waited for: 11 -> 5; matrix products, arithmetic and copies ran while one was open for 12% -> 4% of each run, Pallas kernels for 6% -> 16%
where the time goes in v2:
time: 254 us; the launch traced here: 253 us
  Pallas kernels  114 us (45%)
  waiting for transfers between devices  53.7 us (21%)
  starting transfers between devices  33.4 us (13%)
  blocking collectives  23.1 us (9%)
  local copies, waits for them, and re-layouts  16.7 us (7%)
  matrix products  7.73 us (3%)
    pallas_call x1, Pallas kernels, scatter_teacher(): pl.pallas_call(functools.partial(scatter_kernel, count), out_shape=[jax.S...  74.4 us
    all_to_all x5, waiting for transfers between devices, exchanged(): return lax.all_to_all(blocks, axis, split_axis=0, concat_axis=0, tiled=True)  42 us
    all_to_all x5, starting transfers between devices, exchanged(): return lax.all_to_all(blocks, axis, split_axis=0, concat_axis=0, tiled=True)  27.4 us
    all_to_all x1, blocking collectives, exchanged(): return lax.all_to_all(blocks, axis, split_axis=0, concat_axis=0, tiled=True)  23.1 us
    pallas_call x1, Pallas kernels, student_step(): pl.pallas_call(functools.partial(student_kernel, step_rows, 1.0 / math.sq...  20.8 us
    pallas_call x2, Pallas kernels, teacher_attention(): pl.pallas_call(functools.partial(teacher_kernel, step_rows), out_shape=ja...  18.5 us
    all_to_all x1, waiting for transfers between devices, body(): lax.all_to_all(student_local, 'seq', split_axis=0, concat_axis=1, tiled=T...  11.7 us
    unnamed x28, local copies, waits for them, and re-layouts  8.08 us
  transfers between devices with their start and end apart: 7, of which 5 were waited for; matrix products, arithmetic and copies ran while one was open for 4% of the time, Pallas kernels for 16%

profile of v2, /device:TPU:0, one launch (start us, length us, event | category | flops | bytes accessed | tf_op | source)
XLA Modules:
  0.0 252.9 jit_solution(3632698547730338492)
XLA Ops:
  0.6 0.0 copy-start
  0.6 0.0 copy-start.10
  0.7 0.0 copy-start.11
  0.7 0.0 copy-start.12
  0.7 1.9 fusion.4
  2.6 1.8 fusion
  4.4 0.0 copy-done.10
  4.4 1.6 fusion.2
  6.0 0.0 copy-done.11
  6.0 0.0 copy-done.12
  6.1 0.6 fusion.16
  8.0 74.4 %scatter.1 = (bf16[2,1024,256]{2,1,0:T(8,128)(2,1)}, bf16[2,1024,256]{2,1,0:T(8,128)(2,1)}, bf16[2,1024,256]{2,1,0:T(8,128)(2,1)}, bf16[1024,256]{1,0:T(8,128)(2...) custom-call(bf16[2,128,2048]{2,1,0:T(8,128)(2,1)} %bitcast.48, bf16[2,128,2048]{2,1,0:T(8,128)(2,1)} %bitcast.49, ...), custom_call_target="tpu_custom_call" | custom-call | bytes 6291456 | tf_op jit(solution)/shard_map/scatter/pallas_call | solution.py:311
  82.4 0.1 fusion.12
  82.6 0.1 copy.28
  82.7 1.0 broadcast_in_dim.11
  83.7 10.5 %all-to-all-start = ((bf16[8,128,384]{2,1,0:T(8,128)(2,1)}), bf16[8,128,384]{2,1,0:T(8,128)(2,1)S(1)}, u32[]{:S(2)}, u32[]{:S(2)}) async-start(bf16[8,128,384]{2,1,0:T(8,128)(2,1)} %broadcast_in_dim.11), calls=%async_computation | async-start | bytes 1572864 | tf_op jit(solution)/shard_map/all_to_all | solution.py:336
  94.1 0.0 copy-start.1
  94.1 2.4 copy.27
  96.5 16.6 %all-to-all-done = bf16[8,128,384]{2,1,0:T(8,128)(2,1)S(1)} async-done(((bf16[8,128,384]{2,1,0:T(8,128)(2,1)}), bf16[8,128,384]{2,1,0:T(8,128)(2,1)S(1)}, u32[]{:S(2)}, u32[]{:S(2)}) %all-to-all-start) | async-done | bytes 786464 | tf_op jit(solution)/shard_map/all_to_all | solution.py:336
  113.1 2.1 copy.29
  115.2 4.2 %all-to-all-start.1 = ((bf16[8,128,384]{1,2,0:T(8,128)(2,1)}), bf16[8,128,384]{1,2,0:T(8,128)(2,1)}, u32[]{:S(2)}, u32[]{:S(2)}) async-start(bf16[8,128,384]{1,2,0:T(8,128)(2,1)} %bitcast.45), calls=%async_computation.1 | async-start | bytes 1572864 | tf_op jit(solution)/shard_map/all_to_all | solution.py:336
  119.4 0.6 fusion.15
  120.0 0.0 copy-done.1
  120.0 0.0 copy-start.3
  120.0 1.2 copy-done.3
  121.2 0.0 copy-start.5
  121.2 1.2 copy-done.5
  122.5 9.5 %teacher.3 = bf16[1024,256]{1,0:T(8,128)(2,1)} custom-call(s32[1]{0:T(128)} %bitcast.13.half_ref, f32[1]{0:T(128)} %get-tuple-element.50.weight_ref, bf16[2,1024,256]{2,1,0:T(8,128)(2,1)S(1)} %copy-done.1, bf16[2,1024,256]{2,1,0:T(8,128)(2,1)S(1)} %copy-done.3, bf16[2,1024,256]{2,1,0:T(8,128)(2,1)S(1)} %copy-done.5), custom_call_target="tpu_custom_call" | custom-call | flops 1073741824 | bytes 2097152 | tf_op jit(solution)/shard_map/teacher/pallas_call | solution.py:58
  131.9 2.5 collective-permute-start
  134.4 0.0 copy-start.2
  134.4 0.0 copy-start.4
  134.4 1.3 copy-done.4
  135.7 1.2 copy-done.6
  137.0 9.0 %teacher.2.target_own = bf16[1024,256]{1,0:T(8,128)(2,1)S(1)} custom-call(s32[1]{0:T(128)} %bitcast.half_ref.cfg_ref, f32[1]{0:T(128)} %get-tuple-element.51.weight_ref, bf16[2,1024,256]{2,1,0:T(8,128)(2,1)S(1)} %copy-done.1, bf16[2,1024,256]{2,1,0:T(8,128)(2,1)S(1)} %copy-done.4, bf16[2,1024,256]{2,1,0:T(8,128)(2,1)S(1)} %copy-done.6), custom_call_target="tpu_custom_call" | custom-call | flops 1073741824 | bytes 2097152 | tf_op jit(solution)/shard_map/teacher/pallas_call | solution.py:58
  146.0 0.0 copy-done
  146.0 0.0 collective-permute-done.target_sent
  146.0 0.0 copy-done.2
  146.0 0.0 copy-done.7
  146.1 0.0 copy-done.8
  146.1 0.0 copy-done.9
  146.1 20.8 %student.1 = (bf16[1024,256]{1,0:T(8,128)(2,1)}, bf16[3,128,256]{2,1,0:T(8,128)(2,1)S(1)}, bf16[1024,384]{1,0:T(8,128)(2,1)}) custom-call(s32[1]{0:T(128)} %bitcast.half_ref.cfg_ref, bf16[2,1024,256]{2,1,0:T(8,128)(2,1)S(1)} %copy-done.2, bf16[2,1024,256]{2,1,0:T(8,128)(2,1)} %get-tuple-element.26.key_ref.own_key, ...), custom_call_target="tpu_custom_call" | custom-call | flops 3221225472 | bytes 6291456 | tf_op jit(solution)/shard_map/student/pallas_call | solution.py:175
  166.8 0.0 all-to-all-done.1
  166.8 1.5 copy.30
  168.3 5.9 %all-to-all-start.3 = ((bf16[8,128,384]{2,1,0:T(8,128)(2,1)}), bf16[8,128,384]{2,1,0:T(8,128)(2,1)S(1)}, u32[]{:S(2)}, u32[]{:S(2)}) async-start(bf16[8,128,384]{2,1,0:T(8,128)(2,1)} %bitcast.19), calls=%async_computation.3 | async-start | bytes 1572864 | tf_op jit(solution)/shard_map/all_to_all | solution.py:336
  174.2 0.7 copy.37
  174.9 17.9 %all-to-all-done.3 = bf16[8,128,384]{2,1,0:T(8,128)(2,1)S(1)} async-done(((bf16[8,128,384]{2,1,0:T(8,128)(2,1)}), bf16[8,128,384]{2,1,0:T(8,128)(2,1)S(1)}, u32[]{:S(2)}, u32[]{:S(2)}) %all-to-all-start.3) | async-done | bytes 786464 | tf_op jit(solution)/shard_map/all_to_all | solution.py:336
  192.8 3.4 %all-to-all-start.6 = ((bf16[4,3,32,256]{3,2,1,0:T(8,128)(2,1)}), bf16[4,3,32,256]{3,2,1,0:T(8,128)(2,1)S(1)}, u32[]{:S(2)}, u32[]{:S(2)}) async-start(bf16[4,3,32,256]{3,2,1,0:T(8,128)(2,1)} %bitcast.53), calls=%async_computation.6 | async-start | bytes 393216 | tf_op jit(solution)/shard_map/all_to_all | solution.py:336
  196.2 0.8 convert_reduce_fusion
  197.0 1.1 copy.32
  198.0 0.1 multiply_convert_fusion
  198.1 0.1 copy.33
  198.3 3.2 %all-to-all-done.6 = bf16[4,3,32,256]{3,2,1,0:T(8,128)(2,1)S(1)} async-done(((bf16[4,3,32,256]{3,2,1,0:T(8,128)(2,1)}), bf16[4,3,32,256]{3,2,1,0:T(8,128)(2,1)S(1)}, u32[]{:S(2)}, u32[]{:S(2)}) %all-to-all-start.6) | async-done | bytes 196640 | tf_op jit(solution)/shard_map/all_to_all | solution.py:336
  201.5 0.1 broadcast_in_dim.28
  201.5 23.1 %all_to_all.46 = bf16[8,128,384]{2,1,0:T(8,128)(2,1)} all-to-all(bf16[8,128,384]{2,1,0:T(8,128)(2,1)S(1)} %broadcast_in_dim.28), channel_id=1, replica_groups=mesh['cfg'=2,'seq'=8,'dp'=2] {'seq'}, dimensions={0} | all-to-all | bytes 1572864 | tf_op jit(solution)/shard_map/all_to_all | solution.py:336
  224.6 3.6 %all-to-all-start.2 = ((bf16[8,128,256]{2,1,0:T(8,128)(2,1)}), bf16[8,128,256]{2,1,0:T(8,128)(2,1)S(1)}, u32[]{:S(2)}, u32[]{:S(2)}) async-start(bf16[8,128,256]{2,1,0:T(8,128)(2,1)} %bitcast.17), calls=%async_computation.2 | async-start | bytes 1048576 | tf_op jit(solution)/shard_map/all_to_all | solution.py:418
  228.2 2.4 convolution_convert_fusion
  230.6 11.7 %all-to-all-done.2 = bf16[8,128,256]{2,1,0:T(8,128)(2,1)S(1)} async-done(((bf16[8,128,256]{2,1,0:T(8,128)(2,1)}), bf16[8,128,256]{2,1,0:T(8,128)(2,1)S(1)}, u32[]{:S(2)}, u32[]{:S(2)}) %all-to-all-start.2) | async-done | bytes 524320 | tf_op jit(solution)/shard_map/all_to_all | solution.py:418
  242.3 3.5 %all-to-all-start.5 = ((bf16[4,96,384]{2,1,0:T(8,128)(2,1)}), bf16[4,96,384]{2,1,0:T(8,128)(2,1)S(1)}, u32[]{:S(2)}, u32[]{:S(2)}) async-start(bf16[4,96,384]{2,1,0:T(8,128)(2,1)} %bitcast.21), calls=%async_computation.5 | async-start | bytes 589824 | tf_op jit(solution)/shard_map/all_to_all | solution.py:336
  245.7 0.7 convert_reduce_fusion.2
  246.4 0.3 copy.31
  246.7 1.0 broadcast_in_dim.13
  247.7 4.3 %all-to-all-done.5 = bf16[4,96,384]{2,1,0:T(8,128)(2,1)S(1)} async-done(((bf16[4,96,384]{2,1,0:T(8,128)(2,1)}), bf16[4,96,384]{2,1,0:T(8,128)(2,1)S(1)}, u32[]{:S(2)}, u32[]{:S(2)}) %all-to-all-start.5) | async-done | bytes 294944 | tf_op jit(solution)/shard_map/all_to_all | solution.py:336
  252.1 0.1 reshape.96
  252.2 0.7 copy.35
  (11 shorter events, 0.2 us)
Async XLA Ops:
  0.6 145.3 %copy-start = (bf16[3,128,2048]{2,1,0:T(8,128)(2,1)S(1)}, bf16[3,128,2048]{2,1,0:T(8,128)(2,1)}, u32[]{:S(2)}) copy-start(bf16[3,128,2048]{2,1,0:T(8,128)(2,1)} %param.13) | copy-start | bytes 4718596
  0.6 3.8 %copy-start.10 = (bf16[1,1,128,3072]{3,2,1,0:T(8,128)(2,1)S(1)}, bf16[1,1,128,3072]{3,2,1,0:T(8,128)(2,1)}, u32[]{:S(2)}) copy-start(bf16[1,1,128,3072]{3,2,1,0:T(8,128)(2,1)} %param.11) | copy-start | bytes 2359300
  0.7 5.4 %copy-start.11 = (s32[2,1]{0,1:T(1,128)S(1)}, s32[2,1]{0,1:T(1,128)}, u32[]{:S(2)}) copy-start(s32[2,1]{0,1:T(1,128)} %param.15) | copy-start | bytes 28
  0.7 5.4 %copy-start.12 = (s32[2,1]{0,1:T(1,128)S(1)}, s32[2,1]{0,1:T(1,128)}, u32[]{:S(2)}) copy-start(s32[2,1]{0,1:T(1,128)} %param.14) | copy-start | bytes 28
  83.7 29.4 %all-to-all-start = ((bf16[8,128,384]{2,1,0:T(8,128)(2,1)}), bf16[8,128,384]{2,1,0:T(8,128)(2,1)S(1)}, u32[]{:S(2)}, u32[]{:S(2)}) async-start(bf16[8,128,384]{2,1,0:T(8,128)(2,1)} %broadcast_in_dim.11), calls=%async_computation | async-start | bytes 1572864 | tf_op jit(solution)/shard_map/all_to_all | solution.py:336
  94.1 25.9 %copy-start.1 = (bf16[2,1024,256]{2,1,0:T(8,128)(2,1)S(1)}, bf16[2,1024,256]{2,1,0:T(8,128)(2,1)}, u32[]{:S(2)}) copy-start(bf16[2,1024,256]{2,1,0:T(8,128)(2,1)} %get-tuple-element.25.query_ref.own_query) | copy-start | bytes 3145732
  115.2 51.7 %all-to-all-start.1 = ((bf16[8,128,384]{1,2,0:T(8,128)(2,1)}), bf16[8,128,384]{1,2,0:T(8,128)(2,1)}, u32[]{:S(2)}, u32[]{:S(2)}) async-start(bf16[8,128,384]{1,2,0:T(8,128)(2,1)} %bitcast.45), calls=%async_computation.1 | async-start | bytes 1572864 | tf_op jit(solution)/shard_map/all_to_all | solution.py:336
  120.0 1.2 copy-start.3
  121.2 1.2 copy-start.5
  131.9 14.1 %collective-permute-start = (bf16[1024,256]{1,0:T(8,128)(2,1)}, bf16[1024,256]{1,0:T(8,128)(2,1)}, u32[]{:S(2)}, u32[]{:S(2)}) collective-permute-start(bf16[1024,256]{1,0:T(8,128)(2,1)} %teacher.3), channel_id=1, source_target_pairs={{0,16},{16,0},{1,17},{17,1},{2,18},{18,2},{3,19},{19,3},{4,20},{20... | collective-permute-start | bytes 1572872 | tf_op jit(solution)/shard_map/ppermute | solution.py:399
  134.4 11.6 %copy-start.2 = (bf16[2,1024,256]{2,1,0:T(8,128)(2,1)S(1)}, bf16[2,1024,256]{2,1,0:T(8,128)(2,1)}, u32[]{:S(2)}) copy-start(bf16[2,1024,256]{2,1,0:T(8,128)(2,1)} %get-tuple-element.25.query_ref.own_query) | copy-start | bytes 3145732
  134.4 1.3 copy-start.4
  135.7 1.2 copy-start.6
  136.9 9.1 %copy-start.7 = (bf16[1024,256]{1,0:T(8,128)(2,1)S(1)}, bf16[1024,256]{1,0:T(8,128)(2,1)}, u32[]{:S(2)}) copy-start(bf16[1024,256]{1,0:T(8,128)(2,1)} %get-tuple-element.28.sent_query) | copy-start | bytes 1572868
  136.9 9.1 %copy-start.8 = (bf16[1024,256]{1,0:T(8,128)(2,1)S(1)}, bf16[1024,256]{1,0:T(8,128)(2,1)}, u32[]{:S(2)}) copy-start(bf16[1024,256]{1,0:T(8,128)(2,1)} %get-tuple-element.29.sent_key) | copy-start | bytes 1572868
  137.0 9.1 %copy-start.9 = (bf16[1024,256]{1,0:T(8,128)(2,1)S(1)}, bf16[1024,256]{1,0:T(8,128)(2,1)}, u32[]{:S(2)}) copy-start(bf16[1024,256]{1,0:T(8,128)(2,1)} %get-tuple-element.30.sent_value) | copy-start | bytes 1572868
  168.3 24.5 %all-to-all-start.3 = ((bf16[8,128,384]{2,1,0:T(8,128)(2,1)}), bf16[8,128,384]{2,1,0:T(8,128)(2,1)S(1)}, u32[]{:S(2)}, u32[]{:S(2)}) async-start(bf16[8,128,384]{2,1,0:T(8,128)(2,1)} %bitcast.19), calls=%async_computation.3 | async-start | bytes 1572864 | tf_op jit(solution)/shard_map/all_to_all | solution.py:336
  192.8 8.6 %all-to-all-start.6 = ((bf16[4,3,32,256]{3,2,1,0:T(8,128)(2,1)}), bf16[4,3,32,256]{3,2,1,0:T(8,128)(2,1)S(1)}, u32[]{:S(2)}, u32[]{:S(2)}) async-start(bf16[4,3,32,256]{3,2,1,0:T(8,128)(2,1)} %bitcast.53), calls=%async_computation.6 | async-start | bytes 393216 | tf_op jit(solution)/shard_map/all_to_all | solution.py:336
  224.6 17.7 %all-to-all-start.2 = ((bf16[8,128,256]{2,1,0:T(8,128)(2,1)}), bf16[8,128,256]{2,1,0:T(8,128)(2,1)S(1)}, u32[]{:S(2)}, u32[]{:S(2)}) async-start(bf16[8,128,256]{2,1,0:T(8,128)(2,1)} %bitcast.17), calls=%async_computation.2 | async-start | bytes 1048576 | tf_op jit(solution)/shard_map/all_to_all | solution.py:418
  242.3 9.8 %all-to-all-start.5 = ((bf16[4,96,384]{2,1,0:T(8,128)(2,1)}), bf16[4,96,384]{2,1,0:T(8,128)(2,1)S(1)}, u32[]{:S(2)}, u32[]{:S(2)}) async-start(bf16[4,96,384]{2,1,0:T(8,128)(2,1)} %bitcast.21), calls=%async_computation.5 | async-start | bytes 589824 | tf_op jit(solution)/shard_map/all_to_all | solution.py:336

commit v3 on v2

--- a/solution.py
+++ b/solution.py
@@ -14,7 +14,7 @@
 TSTEPS = 1000
 FACTOR = HDIM ** (-0.5)
 FACTOR_BASE2 = FACTOR * math.log2(math.e)
-VMEM_LIMIT = 48 * 1024 * 1024
+VMEM_LIMIT = 60 * 1024 * 1024
 
 NT = (((1,), (1,)), ((), ()))
 TN = (((0,), (0,)), ((), ()))
@@ -332,6 +332,159 @@
     return outs[0:3], outs[3:6]
 
 
+def tail_kernel(
+    count,
+    dp_count,
+    back_ref,
+    student_ref,
+    up_ref,
+    modulation_ref,
+    tokens_ref,
+    grad_up_ref,
+    rows_ref,
+    parts,
+    up_parts,
+    kept,
+    mine,
+    send_sem,
+    recv_sem,
+    up_send_sem,
+    up_recv_sem,
+    local_sem,
+):
+    me = lax.axis_index("seq")
+    groups = 2 * dp_count
+    group = lax.axis_index("cfg") * dp_count + lax.axis_index("dp")
+    tok_here = mine.shape[0]
+    columns = student_ref.shape[1]
+
+    def rows_of(device):
+        return pl.ds(pl.multiple_of(device * tok_here, tok_here), tok_here)
+
+    own_columns = pl.ds(pl.multiple_of(me * columns, columns), columns)
+
+    def group_device(step):
+        peer = lax.rem(group + step, groups)
+        return {"cfg": peer // dp_count, "dp": lax.rem(peer, dp_count)}
+
+    own_loads = [
+        pltpu.make_async_copy(back_ref.at[rows_of(me), :], parts.at[0], local_sem.at[0]),
+        pltpu.make_async_copy(student_ref.at[rows_of(me), :], kept, local_sem.at[1]),
+        pltpu.make_async_copy(up_ref.at[group], up_parts.at[0], local_sem.at[2]),
+    ]
+    for load in own_loads:
+        load.start()
+
+    barrier = pltpu.get_barrier_semaphore()
+    for step in range(1, count):
+        pl.semaphore_signal(
+            barrier,
+            inc=1,
+            device_id={"seq": lax.rem(me + step, count)},
+            device_id_type=pl.DeviceIdType.MESH,
+        )
+    for step in range(1, groups):
+        pl.semaphore_signal(
+            barrier, inc=1, device_id=group_device(step), device_id_type=pl.DeviceIdType.MESH
+        )
+    pl.semaphore_wait(barrier, count + groups - 2)
+
+    def remote(kind, step):
+        peer = lax.rem(me + step, count)
+        source, target = (
+            (back_ref.at[rows_of(peer), :], parts.at[step]),
+            (student_ref.at[rows_of(peer), :], tokens_ref.at[:, own_columns]),
+            (mine, rows_ref.at[rows_of(me), :]),
+        )[kind]
+        return pltpu.make_async_remote_copy(
+            src_ref=source,
+            dst_ref=target,
+            send_sem=send_sem.at[kind, step],
+            recv_sem=recv_sem.at[kind, step],
+            device_id={"seq": peer},
+            device_id_type=pl.DeviceIdType.MESH,
+        )
+
+    def up_remote(step):
+        return pltpu.make_async_remote_copy(
+            src_ref=up_ref.at[lax.rem(group + step, groups)],
+            dst_ref=up_parts.at[step],
+            send_sem=up_send_sem.at[step],
+            recv_sem=up_recv_sem.at[step],
+            device_id=group_device(step),
+            device_id_type=pl.DeviceIdType.MESH,
+        )
+
+    for step in range(1, count):
+        remote(0, step).start()
+    for step in range(1, groups):
+        up_remote(step).start()
+    for step in range(1, count):
+        remote(1, step).start()
+    for load in own_loads:
+        load.wait()
+    own_store = pltpu.make_async_copy(kept, tokens_ref.at[:, own_columns], local_sem.at[3])
+    own_store.start()
+
+    total = parts[0].astype(jnp.float32)
+    for step in range(1, count):
+        remote(0, step).wait_recv()
+        total = total + parts[step].astype(jnp.float32)
+    low_grad = (total * modulation_ref[...]).astype(jnp.bfloat16)
+    mine[...] = low_grad
+    rows_ref[rows_of(me), :] = low_grad
+    for step in range(1, count):
+        remote(2, step).start()
+
+    up_total = up_parts[0].astype(jnp.float32)
+    for step in range(1, groups):
+        up_remote(step).wait()
+        up_total = up_total + up_parts[step].astype(jnp.float32)
+    grad_up_ref[...] = up_total
+
+    own_store.wait()
+    for step in range(1, count):
+        remote(0, step).wait_send()
+        remote(1, step).wait()
+        remote(2, step).wait()
+
+
+def tail_exchange(back_partial, student_local, up_blocks, modulation):
+    count = lax.axis_size("seq")
+    dp_count = lax.axis_size("dp")
+    length, ranks = back_partial.shape
+    columns = student_local.shape[1]
+    tok_here = length // count
+    any_spec = pl.BlockSpec(memory_space=pl.ANY)
+    vmem_spec = pl.BlockSpec(memory_space=pltpu.VMEM)
+    return pl.pallas_call(
+        functools.partial(tail_kernel, count, dp_count),
+        out_shape=(
+            jax.ShapeDtypeStruct((tok_here, columns * count), jnp.bfloat16),
+            jax.ShapeDtypeStruct(up_blocks.shape[1:], jnp.float32),
+            jax.ShapeDtypeStruct((length, ranks), jnp.bfloat16),
+        ),
+        in_specs=[any_spec, any_spec, any_spec, vmem_spec],
+        out_specs=(any_spec, vmem_spec, vmem_spec),
+        scratch_shapes=[
+            pltpu.VMEM((count, tok_here, ranks), jnp.bfloat16),
+            pltpu.VMEM(up_blocks.shape, jnp.bfloat16),
+            pltpu.VMEM((tok_here, columns), jnp.bfloat16),
+            pltpu.VMEM((tok_here, ranks), jnp.bfloat16),
+            pltpu.SemaphoreType.DMA((3, count)),
+            pltpu.SemaphoreType.DMA((3, count)),
+            pltpu.SemaphoreType.DMA((2 * dp_count,)),
+            pltpu.SemaphoreType.DMA((2 * dp_count,)),
+            pltpu.SemaphoreType.DMA((4,)),
+        ],
+        compiler_params=pltpu.CompilerParams(collective_id=1, has_side_effects=True),
+        cost_estimate=pl.CostEstimate(
+            flops=0, bytes_accessed=8 * length * ranks, transcendentals=0
+        ),
+        name="tail",
+    )(back_partial, student_local, up_blocks, modulation)
+
+
 def exchanged(blocks, axis):
     return lax.all_to_all(blocks, axis, split_axis=0, concat_axis=0, tiled=True)
 
@@ -412,16 +565,12 @@
     student_local, up_partial, back_partial, column_block = lax.optimization_barrier(
         (student_local, up_partial, back_partial, column_block)
     )
-    back_parts = exchanged(back_partial.reshape(seq_count, tok_here, ranks), "seq")
-    rank_backward = jnp.sum(back_parts.astype(jnp.float32), axis=0)
-    low_grad = (rank_backward * modulation).astype(jnp.bfloat16)
-    student_tokens = lax.all_to_all(student_local, "seq", split_axis=0, concat_axis=1, tiled=True)
-    grad_rows = gathered(low_grad, "seq").reshape(length, ranks)
-
     groups = 2 * dp_count
     up_rows = ADAPTER_RANK // groups
-    up_parts = up_partial.reshape(3, groups, up_rows, columns).transpose(1, 0, 2, 3)
-    grad_up = jnp.sum(exchanged(up_parts, ("cfg", "dp")).astype(jnp.float32), axis=0)
+    up_blocks = up_partial.reshape(3, groups, up_rows, columns).transpose(1, 0, 2, 3)
+    student_tokens, grad_up, grad_rows = tail_exchange(
+        back_partial, student_local, up_blocks, modulation
+    )
 
     column_partial = lax.dot_general(
         column_block, grad_rows, TN, preferred_element_type=jnp.float32

time: 254 us -> 234 us (0.921)
  Pallas kernels: 114 us -> 165 us
  waiting for transfers between devices: 53.7 us -> 25 us
  blocking collectives: 23.1 us -> 0 us
  starting transfers between devices: 33.4 us -> 19.9 us
  local copies, waits for them, and re-layouts: 16.7 us -> 10.5 us
    pallas_call x0 -> x1, Pallas kernels: none -> 48 us  [tail_exchange(): pl.pallas_call(functools.partial(tail_kernel, count, dp_count), out_shape...]
    all_to_all x1 -> x0, blocking collectives: 23.1 us -> none  [exchanged(): return lax.all_to_all(blocks, axis, split_axis=0, concat_axis=0, tiled=True)]
    all_to_all x5 -> x3, waiting for transfers between devices: 42 us -> 25 us  [exchanged(): return lax.all_to_all(blocks, axis, split_axis=0, concat_axis=0, tiled=True)]
    all_to_all x1 -> x0, waiting for transfers between devices: 11.7 us -> none  [body(): lax.all_to_all(student_local, 'seq', split_axis=0, concat_axis=1, tiled=T...]
    all_to_all x5 -> x3, starting transfers between devices: 27.4 us -> 17.5 us  [exchanged(): return lax.all_to_all(blocks, axis, split_axis=0, concat_axis=0, tiled=True)]
    all_to_all x1 -> x0, starting transfers between devices: 3.59 us -> none  [body(): lax.all_to_all(student_local, 'seq', split_axis=0, concat_axis=1, tiled=T...]
    unnamed x28 -> x18, local copies, waits for them, and re-layouts: 8.08 us -> 5.01 us
  transfers between devices with their start and end apart: 7 -> 4, of which waited for: 5 -> 2; matrix products, arithmetic and copies ran while one was open for 4% -> 1% of each run, Pallas kernels for 16% -> 18%
where the time goes in v3:
time: 234 us; the launch traced here: 231 us
  Pallas kernels  165 us (71%)
  waiting for transfers between devices  25 us (11%)
  starting transfers between devices  19.9 us (9%)
  local copies, waits for them, and re-layouts  10.5 us (4%)
  matrix products  7.8 us (3%)
    pallas_call x1, Pallas kernels, scatter_teacher(): pl.pallas_call(functools.partial(scatter_kernel, count), out_shape=[jax.S...  74.4 us
    pallas_call x1, Pallas kernels, tail_exchange(): pl.pallas_call(functools.partial(tail_kernel, count, dp_count), out_shape...  48 us
    all_to_all x3, waiting for transfers between devices, exchanged(): return lax.all_to_all(blocks, axis, split_axis=0, concat_axis=0, tiled=True)  25 us
    pallas_call x1, Pallas kernels, student_step(): pl.pallas_call(functools.partial(student_kernel, step_rows, 1.0 / math.sq...  21.7 us
    pallas_call x2, Pallas kernels, teacher_attention(): pl.pallas_call(functools.partial(teacher_kernel, step_rows), out_shape=ja...  20.7 us
    all_to_all x3, starting transfers between devices, exchanged(): return lax.all_to_all(blocks, axis, split_axis=0, concat_axis=0, tiled=True)  17.5 us
    dot_general x3, matrix products, dot_f32(): return jnp.dot(left, right, preferred_element_type=jnp.float32)  5.31 us
    unnamed x18, local copies, waits for them, and re-layouts  5.01 us
  transfers between devices with their start and end apart: 4, of which 2 were waited for; matrix products, arithmetic and copies ran while one was open for 1% of the time, Pallas kernels for 18%

profile of v3, /device:TPU:0, one launch (start us, length us, event | category | flops | bytes accessed | tf_op | source)
XLA Modules:
  0.0 231.0 jit_solution(14542670826448935256)
XLA Ops:
  0.6 0.0 copy-start
  0.6 0.0 copy-start.1
  0.7 0.0 copy-start.4
  0.7 0.0 copy-start.5
  0.7 1.9 fusion.4
  2.6 1.8 fusion
  4.4 0.0 copy-done.1
  4.4 1.6 fusion.2
  6.0 0.0 copy-done.4
  6.1 0.0 copy-done.5
  6.1 0.6 fusion.16
  8.0 74.4 %scatter.1 = (bf16[2,1024,256]{2,1,0:T(8,128)(2,1)}, bf16[2,1024,256]{2,1,0:T(8,128)(2,1)}, bf16[2,1024,256]{2,1,0:T(8,128)(2,1)}, bf16[1024,256]{1,0:T(8,128)(2...) custom-call(bf16[2,128,2048]{2,1,0:T(8,128)(2,1)} %bitcast.47, bf16[2,128,2048]{2,1,0:T(8,128)(2,1)} %bitcast.48, ...), custom_call_target="tpu_custom_call" | custom-call | bytes 6291456 | tf_op jit(solution)/shard_map/scatter/pallas_call | solution.py:311
  82.5 0.1 fusion.12
  82.6 0.1 copy.18
  82.7 1.0 broadcast_in_dim.9
  83.7 10.5 %all-to-all-start = ((bf16[8,128,384]{2,1,0:T(8,128)(2,1)}), bf16[8,128,384]{2,1,0:T(8,128)(2,1)}, u32[]{:S(2)}, u32[]{:S(2)}) async-start(bf16[8,128,384]{2,1,0:T(8,128)(2,1)} %broadcast_in_dim.9), calls=%async_computation | async-start | bytes 1572864 | tf_op jit(solution)/shard_map/all_to_all | solution.py:489
  94.2 0.4 copy.17
  94.6 18.7 %all-to-all-done = bf16[8,128,384]{2,1,0:T(8,128)(2,1)} async-done(((bf16[8,128,384]{2,1,0:T(8,128)(2,1)}), bf16[8,128,384]{2,1,0:T(8,128)(2,1)}, u32[]{:S(2)}, u32[]{:S(2)}) %all-to-all-start) | async-done | bytes 786464 | tf_op jit(solution)/shard_map/all_to_all | solution.py:489
  113.2 1.0 copy.19
  114.2 3.5 %all-to-all-start.1 = ((bf16[8,128,384]{1,2,0:T(8,128)(2,1)}), bf16[8,128,384]{1,2,0:T(8,128)(2,1)S(1)}, u32[]{:S(2)}, u32[]{:S(2)}) async-start(bf16[8,128,384]{1,2,0:T(8,128)(2,1)} %bitcast.15), calls=%async_computation.1 | async-start | bytes 1572864 | tf_op jit(solution)/shard_map/all_to_all | solution.py:489
  117.8 0.7 fusion.15
  118.4 10.4 %teacher.3 = bf16[1024,256]{1,0:T(8,128)(2,1)} custom-call(s32[1]{0:T(128)} %bitcast.13.half_ref, f32[1]{0:T(128)} %get-tuple-element.55.weight_ref, bf16[2,1024,256]{2,1,0:T(8,128)(2,1)} %get-tuple-element.28.query_ref.own_query, bf16[2,1024,256]{2,1,0:T(8,128)(2,1)} %get-tuple-element.29.key_ref.own_key, ...), custom_call_target="tpu_custom_call" | custom-call | flops 1073741824 | bytes 2097152 | tf_op jit(solution)/shard_map/teacher/pallas_call | solution.py:58
  128.8 2.5 %collective-permute-start = (bf16[1024,256]{1,0:T(8,128)(2,1)}, bf16[1024,256]{1,0:T(8,128)(2,1)S(1)}, u32[]{:S(2)}, u32[]{:S(2)}) collective-permute-start(bf16[1024,256]{1,0:T(8,128)(2,1)} %teacher.3), channel_id=1, source_target_pairs={{0,16},{16,0},{1,17},{17,1},{2,18},{18,2},{3,19},{19,3},{4,20},{20... | collective-permute-start | bytes 1572872 | tf_op jit(solution)/shard_map/ppermute | solution.py:552
  131.2 0.6 copy.27
  131.8 10.4 %teacher.2.target_own = bf16[1024,256]{1,0:T(8,128)(2,1)} custom-call(s32[1]{0:T(128)} %bitcast.half_ref.cfg_ref, f32[1]{0:T(128)} %get-tuple-element.56.weight_ref, bf16[2,1024,256]{2,1,0:T(8,128)(2,1)} %get-tuple-element.28.query_ref.own_query, bf16[2,1024,256]{2,1,0:T(8,128)(2,1)} %get-tuple-element.29.key_ref.own_key, ...), custom_call_target="tpu_custom_call" | custom-call | flops 1073741824 | bytes 2097152 | tf_op jit(solution)/shard_map/teacher/pallas_call | solution.py:58
  142.2 0.0 copy-done
  142.2 0.7 constant_dynamic-slice_fusion.up_ref
  142.9 0.0 collective-permute-done.target_sent
  142.9 0.0 copy-start.3
  142.9 0.8 copy-done.3
  143.7 21.7 %student.1 = (bf16[1024,256]{1,0:T(8,128)(2,1)}, bf16[3,128,256]{2,1,0:T(8,128)(2,1)}, bf16[1024,384]{1,0:T(8,128)(2,1)}) custom-call(s32[1]{0:T(128)} %bitcast.half_ref.cfg_ref, bf16[2,1024,256]{2,1,0:T(8,128)(2,1)} %get-tuple-element.28.query_ref.own_query, bf16[2,1024,256]{2,1,0:T(8,128)(2,1)} %get-tuple-element.29.key_ref.own_key, ...), custom_call_target="tpu_custom_call" | custom-call | flops 3221225472 | bytes 6291456 | tf_op jit(solution)/shard_map/student/pallas_call | solution.py:175
  165.4 0.0 all-to-all-done.1
  165.4 0.4 copy.20
  165.8 1.6 copy.26
  167.4 48.0 %tail.1 = (bf16[128,2048]{1,0:T(8,128)(2,1)}, f32[3,32,256]{2,1,0:T(8,128)}, bf16[1024,384]{1,0:T(8,128)(2,1)}) custom-call(bf16[1024,384]{1,0:T(8,128)(2,1)} %get-tuple-element.40.back_ref, bf16[1024,256]{1,0:T(8,128)(2,1)} %get-tuple-element.41.student_ref, bf16[4,3,32,256]{3,2,1,0:T(8,128)(2,1)} %bitcast.50, f32[1,384]{1,0:T(1,128)} %bitcast.55), custom_call_target="tpu_custom_call" | custom-call | bytes 3145728 | tf_op jit(solution)/shard_map/tail/pallas_call | solution.py:460
  215.4 0.0 copy-start.2
  215.4 2.5 %convolution_convert_fusion = bf16[384,384]{1,0:T(8,128)(2,1)} fusion(bf16[1024,384]{1,0:T(8,128)(2,1)S(1)} %bitcast.51, bf16[1024,384]{1,0:T(8,128)(2,1)} %get-tuple-element.45), kind=kOutput, calls=%fused_computation | convolution fusion | flops 302137344 | bytes 1867776 | tf_op jit(solution)/shard_map/dot_general | solution.py:575
  217.9 3.5 %all-to-all-start.2 = ((bf16[4,96,384]{2,1,0:T(8,128)(2,1)}), bf16[4,96,384]{2,1,0:T(8,128)(2,1)S(1)}, u32[]{:S(2)}, u32[]{:S(2)}) async-start(bf16[4,96,384]{2,1,0:T(8,128)(2,1)} %bitcast.20), calls=%async_computation.2 | async-start | bytes 589824 | tf_op jit(solution)/shard_map/all_to_all | solution.py:489
  221.4 6.3 %all-to-all-done.2 = bf16[4,96,384]{2,1,0:T(8,128)(2,1)S(1)} async-done(((bf16[4,96,384]{2,1,0:T(8,128)(2,1)}), bf16[4,96,384]{2,1,0:T(8,128)(2,1)S(1)}, u32[]{:S(2)}, u32[]{:S(2)}) %all-to-all-start.2) | async-done | bytes 294944 | tf_op jit(solution)/shard_map/all_to_all | solution.py:489
  227.7 0.1 reshape.64
  227.8 0.7 copy.22
  228.5 1.9 copy.30
  230.4 0.0 copy-done.2
  230.4 0.6 copy.31
  (6 shorter events, 0.1 us)
Async XLA Ops:
  0.6 141.5 %copy-start = (bf16[3,128,2048]{2,1,0:T(8,128)(2,1)S(1)}, bf16[3,128,2048]{2,1,0:T(8,128)(2,1)}, u32[]{:S(2)}) copy-start(bf16[3,128,2048]{2,1,0:T(8,128)(2,1)} %param.13) | copy-start | bytes 4718596
  0.6 3.8 %copy-start.1 = (bf16[1,1,128,3072]{3,2,1,0:T(8,128)(2,1)S(1)}, bf16[1,1,128,3072]{3,2,1,0:T(8,128)(2,1)}, u32[]{:S(2)}) copy-start(bf16[1,1,128,3072]{3,2,1,0:T(8,128)(2,1)} %param.11) | copy-start | bytes 2359300
  0.7 5.4 %copy-start.4 = (s32[2,1]{0,1:T(1,128)S(1)}, s32[2,1]{0,1:T(1,128)}, u32[]{:S(2)}) copy-start(s32[2,1]{0,1:T(1,128)} %param.15) | copy-start | bytes 28
  0.7 5.4 %copy-start.5 = (s32[2,1]{0,1:T(1,128)S(1)}, s32[2,1]{0,1:T(1,128)}, u32[]{:S(2)}) copy-start(s32[2,1]{0,1:T(1,128)} %param.14) | copy-start | bytes 28
  83.7 29.5 %all-to-all-start = ((bf16[8,128,384]{2,1,0:T(8,128)(2,1)}), bf16[8,128,384]{2,1,0:T(8,128)(2,1)}, u32[]{:S(2)}, u32[]{:S(2)}) async-start(bf16[8,128,384]{2,1,0:T(8,128)(2,1)} %broadcast_in_dim.9), calls=%async_computation | async-start | bytes 1572864 | tf_op jit(solution)/shard_map/all_to_all | solution.py:489
  114.2 51.2 %all-to-all-start.1 = ((bf16[8,128,384]{1,2,0:T(8,128)(2,1)}), bf16[8,128,384]{1,2,0:T(8,128)(2,1)S(1)}, u32[]{:S(2)}, u32[]{:S(2)}) async-start(bf16[8,128,384]{1,2,0:T(8,128)(2,1)} %bitcast.15), calls=%async_computation.1 | async-start | bytes 1572864 | tf_op jit(solution)/shard_map/all_to_all | solution.py:489
  128.8 14.1 %collective-permute-start = (bf16[1024,256]{1,0:T(8,128)(2,1)}, bf16[1024,256]{1,0:T(8,128)(2,1)S(1)}, u32[]{:S(2)}, u32[]{:S(2)}) collective-permute-start(bf16[1024,256]{1,0:T(8,128)(2,1)} %teacher.3), channel_id=1, source_target_pairs={{0,16},{16,0},{1,17},{17,1},{2,18},{18,2},{3,19},{19,3},{4,20},{20... | collective-permute-start | bytes 1572872 | tf_op jit(solution)/shard_map/ppermute | solution.py:552
  142.9 0.8 copy-start.3
  215.4 15.0 %copy-start.2 = (f32[3,32,256]{2,1,0:T(8,128)S(1)}, f32[3,32,256]{2,1,0:T(8,128)}, u32[]{:S(2)}) copy-start(f32[3,32,256]{2,1,0:T(8,128)} %get-tuple-element.64) | copy-start | bytes 294916
  217.9 9.8 %all-to-all-start.2 = ((bf16[4,96,384]{2,1,0:T(8,128)(2,1)}), bf16[4,96,384]{2,1,0:T(8,128)(2,1)S(1)}, u32[]{:S(2)}, u32[]{:S(2)}) async-start(bf16[4,96,384]{2,1,0:T(8,128)(2,1)} %bitcast.20), calls=%async_computation.2 | async-start | bytes 589824 | tf_op jit(solution)/shard_map/all_to_all | solution.py:489
